TPU v7x, 32 devices: a whole 2x2x4 slice. The times are simulated.
32 devices in a mesh: grp: 2 (over x), seq: 16 (over z, y, core).
Axes of the slice: x: 2, y: 2, z: 4, core: 2. Of those that a mesh axis runs over, the one named last changes fastest.
Arguments:
- cont_query: bfloat16 [64, 32, 2560], P(('grp', 'seq')), parts along dimension 0, may hold values from -180 to 180
- cont_key: bfloat16 [64, 32, 512], P(('grp', 'seq')), parts along dimension 0, may hold values from -6 to 6
- cont_value: bfloat16 [64, 32, 512], P(('grp', 'seq')), parts along dimension 0, may hold values from -6 to 6
- prefix_key: bfloat16 [4, 2048, 512], P('grp', 'seq'), parts along dimension 0, may hold values from -7 to 7
- prefix_value: bfloat16 [4, 2048, 512], P('grp', 'seq'), parts along dimension 0, may hold values from -6 to 6
- out_weight: bfloat16 [2560, 2560], P(None, 'seq'), may hold values from -0.125 to 0.125
- norm_gain: float32 [2560], replicated, may hold values from 0.5 to 1.5
- lm_head: bfloat16 [2560, 76032], P(None, 'seq'), may hold values from -18 to 18
- target_ids: int32 [64, 32], P(('grp', 'seq')), parts along dimension 0, may hold values from 0 to 76031
- cont_len: int32 [64], P(('grp', 'seq')), parts along dimension 0, may hold values from 8 to 32
- prompt_len: int32 [4], P('grp'), parts along dimension 0, may hold values from 1024 to 2048
- group_of: int32 [64], P('grp'), parts along dimension 0, may hold values from 0 to 1, as said below
- rewards: float32 [64], P(('grp', 'seq')), parts along dimension 0, may hold values from -13 to 13
Outputs:
- token_logprob: float32 [64, 32], P(('grp', 'seq')), parts along dimension 0
- advantage: float32 [64], P(('grp', 'seq')), parts along dimension 0
- objective: float32 [64], P(('grp', 'seq')), parts along dimension 0
There are 2 independent parts, one for each index of `grp`. A program takes and returns all parts, laid end to end along the dimension named above; an argument that names none is the same for every part. Nothing has to cross between parts.
Inputs may be any that keep to these rules, and one draw needn't show every extreme that they name: `group_of`: each of the 2 prompts is named by exactly 16 continuations.
All inputs are finite; a program needn't handle non-finite values.
Results may differ from a plain program's by a relative error of at most 0.0026.
Values may be sent and summed in bfloat16 or wider, within the bound.
A program may use at most 128 MiB of HBM per device.

v0:
```python
import jax
import jax.numpy as jnp
from jax import lax
from jax.sharding import PartitionSpec as P

HD = 128
GROUP = 16


NEGATIVE = -1e30
EPSILON = 1e-06
REWARD_FLOOR = 0.25


def absorb(running, queries, key_rows, value_rows, visible):
    peak_old, sum_old, acc_old = running
    cont_count, length, kv_width = key_rows.shape
    head_count = kv_width // HD
    key_heads = key_rows.reshape(cont_count, length, head_count, HD)
    value_heads = value_rows.reshape(cont_count, length, head_count, HD).astype(jnp.float32)
    scores = jnp.einsum(
        "ctkgd,cnkd->ctkgn", queries, key_heads, preferred_element_type=jnp.float32
    ) * HD ** (-0.5)
    scores = jnp.where(visible, scores, NEGATIVE)
    peak_new = jnp.maximum(peak_old, jnp.max(scores, axis=-1))
    weights = jnp.where(visible, jnp.exp(scores - peak_new[..., None]), 0.0)
    factor = jnp.exp(peak_old - peak_new)
    sum_new = sum_old * factor + jnp.sum(weights, axis=-1)
    acc_new = acc_old * factor[..., None] + jnp.einsum(
        "ctkgn,cnkd->ctkgd", weights, value_heads, precision=lax.Precision.HIGHEST
    )
    return (peak_new, sum_new, acc_new)


def normalize(hidden, norm_gain):
    widened = hidden.astype(jnp.float32)
    factor = lax.rsqrt(jnp.mean(widened * widened, axis=-1, keepdims=True) + EPSILON)
    return (widened * factor * norm_gain).astype(jnp.bfloat16)


def shard_stats(normed, token_ids, head, vocab_offset):
    logits = jnp.dot(normed, head, preferred_element_type=jnp.float32)
    maximum = jnp.max(logits, axis=1)
    total_mass = jnp.sum(jnp.exp(logits - maximum[:, None]), axis=1)
    columns = vocab_offset + jnp.arange(head.shape[1], dtype=jnp.int32)
    picked = jnp.sum(jnp.where(token_ids[:, None] == columns[None, :], logits, 0.0), axis=1)
    return (maximum, total_mass, picked)


def per_device(
    cont_query,
    cont_key,
    cont_value,
    prefix_key,
    prefix_value,
    out_weight,
    norm_gain,
    lm_head,
    target_ids,
    cont_len,
    prompt_len,
    group_of,
    rewards,
):
    cont_count, cont_span, query_width = cont_query.shape
    own_rows = cont_count * cont_span
    kv_width = cont_key.shape[2]
    kv_heads = kv_width // HD
    per_group = query_width // kv_width
    device_index = lax.axis_index("seq")
    own_groups = lax.dynamic_slice_in_dim(group_of, device_index * cont_count, cont_count)
    own_prompt_len = prompt_len[own_groups]
    queries = cont_query.reshape(cont_count, cont_span, kv_heads, per_group, HD)
    shape_stats = (cont_count, cont_span, kv_heads, per_group)
    running = (
        jnp.full(shape_stats, NEGATIVE, jnp.float32),
        jnp.zeros(shape_stats, jnp.float32),
        jnp.zeros(shape_stats + (HD,), jnp.float32),
    )
    position = jnp.arange(cont_span, dtype=jnp.int32)
    causal = (position[None, :] <= position[:, None]).reshape(1, cont_span, 1, 1, cont_span)
    running = absorb(running, queries, cont_key, cont_value, causal)
    key_piece = jnp.take(lax.all_gather(prefix_key, "seq", axis=1, tiled=True), own_groups, axis=0)
    value_piece = jnp.take(
        lax.all_gather(prefix_value, "seq", axis=1, tiled=True), own_groups, axis=0
    )
    length = key_piece.shape[1]
    visible = jnp.arange(length, dtype=jnp.int32)[None, :] < own_prompt_len[:, None]
    running = absorb(
        running, queries, key_piece, value_piece, visible.reshape(cont_count, 1, 1, 1, length)
    )
    attended = (
        (running[2] / running[1][..., None]).astype(jnp.bfloat16).reshape(own_rows, query_width)
    )
    hidden_cols = jnp.dot(
        lax.all_gather(attended, "seq", axis=0, tiled=True),
        out_weight,
        preferred_element_type=jnp.float32,
    ).astype(jnp.bfloat16)
    every_id = lax.all_gather(target_ids.reshape(own_rows), "seq", axis=0, tiled=True)
    vocab_dev = lm_head.shape[1]
    vocab_offset = device_index * vocab_dev
    whole = lax.all_gather(hidden_cols, "seq", axis=1, tiled=True)
    maximum, total_mass, picked = shard_stats(
        normalize(whole, norm_gain), every_id, lm_head, vocab_offset
    )
    shares = (
        lax.all_to_all(maximum[None, :], "seq", split_axis=1, concat_axis=0, tiled=True),
        lax.all_to_all(total_mass[None, :], "seq", split_axis=1, concat_axis=0, tiled=True),
        lax.all_to_all(picked[None, :], "seq", split_axis=1, concat_axis=0, tiled=True),
    )
    maximum = jnp.max(shares[0], axis=0)
    total_mass = jnp.sum(shares[1] * jnp.exp(shares[0] - maximum[None, :]), axis=0)
    picked = jnp.sum(shares[2], axis=0)
    logprob = (picked - maximum - jnp.log(total_mass)).reshape(cont_count, cont_span)
    live = position[None, :] < cont_len[:, None]
    token_logprob = jnp.where(live, logprob, 0.0)
    every_reward = lax.all_gather(rewards, "seq", axis=0, tiled=True)
    own_rows_groups = (own_groups[:, None] == group_of[None, :]).astype(jnp.float32)
    group_mean = jnp.dot(own_rows_groups, every_reward, precision=lax.Precision.HIGHEST) / GROUP
    deviation = every_reward[None, :] - group_mean[:, None]
    spread = jnp.sqrt(jnp.sum(own_rows_groups * deviation * deviation, axis=1) / (GROUP - 1))
    advantage = (rewards - group_mean) / jnp.maximum(spread, REWARD_FLOOR)
    objective = advantage * jnp.sum(token_logprob, axis=1) / cont_len.astype(jnp.float32)
    return (token_logprob, advantage, objective)


def solution(mesh):
    placed = (
        P(("grp", "seq"), None, None),
        P(("grp", "seq"), None, None),
        P(("grp", "seq"), None, None),
        P("grp", "seq", None),
        P("grp", "seq", None),
        P(None, "seq"),
        P(),
        P(None, "seq"),
        P(("grp", "seq"), None),
        P(("grp", "seq")),
        P("grp"),
        P("grp"),
        P(("grp", "seq")),
    )
    return jax.shard_map(
        per_device,
        mesh=mesh,
        in_specs=placed,
        out_specs=(P(("grp", "seq"), None), P(("grp", "seq")), P(("grp", "seq"))),
        check_vma=False,
    )
```

profile of v0, /device:TPU:0, one launch (start us, length us, event | category | flops | bytes accessed | tf_op | source)
XLA Modules:
  0.0 357.9 jit_solution(8549242791594035792)
XLA Ops:
  7.2 0.0 copy-start
  7.2 0.0 all-gather.5.cloned.1.call-start
  7.2 0.7 all-gather.5.cloned.1.call-update
  7.9 0.0 all-gather.7.cloned.1.call-start
  8.0 0.7 all-gather.7.cloned.1.call-update
  8.7 0.0 all-gather.9.cloned.1.call-start
  8.7 1.4 reshape.143
  10.1 0.9 reshape.142
  10.9 0.9 reshape.144
  11.8 1.2 compare_and_fusion
  13.1 1.3 gather_fusion
  14.4 1.4 fusion.56
  15.8 0.1 iota_compare_fusion
  15.9 47.4 %all-gather.5.cloned.1.call-done = bf16[2,2048,512]{2,1,0:T(8,128)(2,1)} async-done(((bf16[2,128,512]{2,1,0:T(8,128)(2,1)}), bf16[2,2048,512]{2,1,0:T(8,128)(2,1)}) %all-gather.5.cloned.1.call-update) | async-done | bytes 4194320 | tf_op jit(solution)/shard_map/all_gather | solution.py:83
  63.3 4.5 %fusion.55 = (bf16[2,1024,512]{2,1,0:T(8,128)(2,1)}, bf16[2,1024,512]{2,1,0:T(8,128)(2,1)}) fusion(bf16[2,2048,512]{2,1,0:T(8,128)(2,1)} %all-gather.5.cloned.1.call-done), kind=kLoop, calls=%fused_computation.85 | loop fusion | bytes 8388608 | tf_op jit(solution)/shard_map/jit(_take)/gather | solution.py:83
  67.8 2.3 gather_fusion.1
  70.1 3.7 %gather_fusion.2 = bf16[2,1024,512]{2,1,0:T(8,128)(2,1)} fusion(bf16[2,1024,512]{2,1,0:T(8,128)(2,1)} %get-tuple-element.17, s32[1024]{0:T(1024)S(1)} %pad_clamp_fusion), kind=kCustom, calls=%fused_computation.1.clone | custom fusion | bytes 4194312 | tf_op jit(solution)/shard_map/jit(_take)/gather | solution.py:83
  73.8 40.7 %all-gather.7.cloned.1.call-done = bf16[2,2048,512]{2,1,0:T(8,128)(2,1)} async-done(((bf16[2,128,512]{2,1,0:T(8,128)(2,1)}), bf16[2,2048,512]{2,1,0:T(8,128)(2,1)}) %all-gather.7.cloned.1.call-update) | async-done | bytes 4194320 | tf_op jit(solution)/shard_map/all_gather | solution.py:85
  114.5 4.5 %fusion.54 = (bf16[2,1024,512]{2,1,0:T(8,128)(2,1)}, bf16[2,1024,512]{2,1,0:T(8,128)(2,1)}) fusion(bf16[2,2048,512]{2,1,0:T(8,128)(2,1)} %all-gather.7.cloned.1.call-done), kind=kLoop, calls=%fused_computation.84 | loop fusion | bytes 8388608 | tf_op jit(solution)/shard_map/jit(_take)/gather | solution.py:84
  119.0 3.6 gather_fusion.3
  122.5 3.6 %gather_fusion.4 = bf16[2,1024,512]{2,1,0:T(8,128)(2,1)} fusion(bf16[2,1024,512]{2,1,0:T(8,128)(2,1)} %get-tuple-element.15, s32[1024]{0:T(1024)S(1)} %pad_clamp_fusion), kind=kCustom, calls=%fused_computation.3.clone | custom fusion | bytes 4194312 | tf_op jit(solution)/shard_map/jit(_take)/gather | solution.py:84
  126.2 6.3 %maximum_select_fusion.1 = (bf16[2,2048,512]{2,1,0:T(8,128)(2,1)}, bf16[2,2048,512]{2,1,0:T(8,128)(2,1)}) fusion(bf16[2,1024,512]{2,1,0:T(8,128)(2,1)} %gather_fusion.4, bf16[2,1024,512]{2,1,0:T(8,128)(2,1)} %gather_fusion.3, pred[2]{0:T(512)(128)(4,1)} %get-tuple-element.12, bf16[2,1024,512]{2,1,0:T(8,128)(2,1)} %gather_fusion.2, ...), kind=kLoop, calls=%fused_computation.29 | loop fusion | flops 20971520 | bytes 16777218 | tf_op jit(solution)/shard_map/jit(_take)/select_n | solution.py:84
  132.5 6.9 %reshape.145 = bf16[2,2048,4,128]{3,2,1,0:T(4,128)(2,1)} reshape(bf16[2,2048,512]{2,1,0:T(8,128)(2,1)} %get-tuple-element.22) | data formatting | bytes 8388608 | tf_op jit(solution)/shard_map/reshape | solution.py:19
  139.4 6.9 %reshape.146 = bf16[2,2048,4,128]{3,2,1,0:T(4,128)(2,1)} reshape(bf16[2,2048,512]{2,1,0:T(8,128)(2,1)} %get-tuple-element.21) | data formatting | bytes 8388608 | tf_op jit(solution)/shard_map/reshape | solution.py:20
  146.4 5.1 %bitcast_reduce_fusion = (f32[2,32,4,5]{1,3,2,0:T(8,128)S(1)}, f32[2,4,2048,32,5]{2,3,4,1,0:T(8,128)S(1)}) fusion(pred[2,2048]{1,0:T(4,128)(4,1)S(1)} %iota_compare_fusion, bf16[2,32,4,5,128]{4,3,2,1,0:T(8,128)(2,1)S(1)} %reshape.143, bf16[2,2048,4,128,1]{3,2,1,0,4:T(4,128)(2,1)} %bitcast.49), kind=kOutput, calls=%fused_computation.13 | convolution fusion | flops 678951680 | bytes 15016960 | tf_op jit(solution)/shard_map/ctkgd,cnkd->ctkgn/dot_general | solution.py:21
  151.5 2.8 fusion.5
  154.3 7.1 %fusion.21 = f32[2,32,4,5,128]{4,1,3,2,0:T(8,128)S(1)} fusion(f32[2,4,2048,32,5]{2,3,4,1,0:T(8,128)S(1)} %get-tuple-element.26, f32[2,32,4,5]{1,3,2,0:T(8,128)S(1)} %get-tuple-element.19, pred[2,2048]{1,0:T(4,128)(4,1)S(1)} %iota_compare_fusion, bf16[2,2048,4,128,1]{3,2,1,0,4:T(4,128)(2,1)S(1)} %bitcast.48), kind=kOutput, calls=%fused_computation.33 | convolution fusion | flops 4037017600 | bytes 15344640 | tf_op jit(solution)/shard_map/ctkgn,cnkd->ctkgd/dot_general | solution.py:29
  161.4 0.2 fusion.34
  161.7 1.3 fusion.32
  163.0 0.0 copy-start.12
  163.0 0.0 copy-start.8
  163.0 0.2 copy.38
  163.2 1.1 reshape.147
  164.3 0.0 all-gather.9.cloned.1.call-update
  164.3 0.3 all-gather.11.cloned.1.call-start
  164.6 54.1 %all-gather.9.cloned.1.call-done = bf16[1024,2560]{1,0:T(8,128)(2,1)} async-done(((bf16[64,2560]{1,0:T(8,128)(2,1)}), bf16[1024,2560]{1,0:T(8,128)(2,1)}) %all-gather.9.cloned.1.call-update) | async-done | bytes 5242896 | tf_op jit(solution)/shard_map/all_gather | solution.py:96
  218.7 5.0 %convolution_convert_fusion = bf16[1024,160]{0,1:T(8,128)(2,1)} fusion(bf16[1024,2560]{1,0:T(8,128)(2,1)} %all-gather.9.cloned.1.call-done, bf16[2560,160]{0,1:T(8,128)(2,1)S(1)} %copy-done), kind=kOutput, calls=%fused_computation.43 | convolution fusion | flops 839024640 | bytes 6389760 | tf_op jit(solution)/shard_map/dot_general | solution.py:95
  223.8 0.0 all-gather.11.cloned.1.call-update
  223.8 0.1 reshape.193
  223.9 0.6 dynamic-slice
  225.8 0.2 dynamic-update-slice
  226.0 0.2 dynamic-update-slice.1
  226.3 32.1 %all-reduce.1 = f32[32]{0:T(128)S(1)} all-reduce(f32[32]{0:T(128)S(1)} %dynamic-update-slice.1), channel_id=1, replica_groups=mesh['grp'=2,'seq'=16] {'seq'}, use_global_device_ids=true, to_apply=%add.1 | all-reduce | flops 32 | bytes 256
  258.4 7.4 %all-reduce = s32[1024]{0:T(1024)S(1)} all-reduce(s32[1024]{0:T(1024)S(1)} %dynamic-update-slice), channel_id=1, replica_groups=mesh['grp'=2,'seq'=16] {'seq'}, use_global_device_ids=true, to_apply=%add | all-reduce | flops 1024 | bytes 8192
  265.8 0.2 fusion.33
  266.0 12.4 %all-gather.11.cloned.1.call-done = bf16[1024,2560]{0,1:T(8,128)(2,1)} async-done(((bf16[1024,160]{0,1:T(8,128)(2,1)}), bf16[1024,2560]{0,1:T(8,128)(2,1)}) %all-gather.11.cloned.1.call-update) | async-done | bytes 5242896 | tf_op jit(solution)/shard_map/all_gather | solution.py:103
  278.4 3.8 %fusion = f32[1024]{0:T(1024)S(1)} fusion(bf16[1024,2560]{0,1:T(8,128)(2,1)} %all-gather.11.cloned.1.call-done), kind=kLoop, calls=%fused_computation.9 | loop fusion | flops 7863296 | bytes 5246976 | tf_op jit(solution)/shard_map/reduce_sum | solution.py:37
  282.2 0.3 copy-done.2
  282.4 30.9 %fusion.57 = (f32[1024]{0:T(1024)S(1)}, f32[1024,4752]{0,1:T(8,128)}) fusion(bf16[2560,4752]{0,1:T(8,128)(2,1)} %param.22, bf16[1024,2560]{0,1:T(8,128)(2,1)S(1)} %copy-done.2, f32[2560]{0:T(1024)S(1)} %copy-done.10, f32[1024]{0:T(1024)S(1)} %add_rsqrt_fusion), kind=kOutput, calls=%fused_computation.87 | convolution fusion | flops 24929517568 | bytes 49055744 | tf_op jit(solution)/shard_map/dot_general | solution.py:42
  313.3 0.7 all_to_all.36
  314.0 3.5 all-to-all-start.1
  317.5 0.0 copy-start.1
  317.5 0.0 copy-start.6
  317.5 9.6 %select_reduce_fusion = (f32[1024]{0:T(1024)S(1)}, f32[1024]{0:T(1024)S(1)}) fusion(f32[1024,4752]{0,1:T(8,128)} %get-tuple-element.28, s32[1024]{0:T(1024)S(1)} %all-reduce, s32[4752]{0:T(1024)S(1)} %iota_add_fusion, f32[1024]{0:T(1024)S(1)} %get-tuple-element.27), kind=kLoop, calls=%fused_computation.6 | loop fusion | flops 24328192 | bytes 19499584 | tf_op jit(solution)/shard_map/reduce_sum | solution.py:46
  327.1 0.7 all_to_all.38
  327.8 6.0 %all-to-all-start.2 = ((f32[1,16,64]{2,0,1:T(1,128)}), f32[1,16,64]{2,0,1:T(1,128)S(1)}, u32[]{:S(2)}, u32[]{:S(2)}) async-start(f32[1,16,64]{2,0,1:T(1,128)} %all_to_all.38), calls=%async_computation.2 | async-start | bytes 16384 | tf_op jit(solution)/shard_map/all_to_all | solution.py:109
  333.7 0.2 fusion.44
  333.9 0.7 all_to_all.34
  334.6 5.5 %all-to-all-done.2 = f32[1,16,64]{2,0,1:T(1,128)S(1)} async-done(((f32[1,16,64]{2,0,1:T(1,128)}), f32[1,16,64]{2,0,1:T(1,128)S(1)}, u32[]{:S(2)}, u32[]{:S(2)}) %all-to-all-start.2) | async-done | bytes 4128 | tf_op jit(solution)/shard_map/all_to_all | solution.py:109
  340.2 3.4 all-to-all-start
  343.6 6.4 %all-to-all-done = f32[1,16,64]{2,0,1:T(1,128)S(1)} async-done(((f32[1,16,64]{2,0,1:T(1,128)}), f32[1,16,64]{2,0,1:T(1,128)S(1)}, u32[]{:S(2)}, u32[]{:S(2)}) %all-to-all-start) | async-done | bytes 4128 | tf_op jit(solution)/shard_map/all_to_all | solution.py:110
  350.0 0.1 sub.92
  350.1 0.7 fusion.53
  350.9 0.5 convert_divide_fusion
  (34 shorter events, 0.2 us)
Async XLA Ops:
  7.2 211.6 %copy-start = (bf16[2560,160]{0,1:T(8,128)(2,1)S(1)}, bf16[2560,160]{0,1:T(8,128)(2,1)}, u32[]{:S(2)}) copy-start(bf16[2560,160]{0,1:T(8,128)(2,1)} %param.20) | copy-start | bytes 2457604
  7.2 56.1 %all-gather.5.cloned.1.call-start = ((), (), s32[]{:S(2)}) async-start(), calls=%async_computation.3 | async-start | bytes 4456448 | tf_op jit(solution)/shard_map/all_gather | solution.py:83
  7.9 106.6 %all-gather.7.cloned.1.call-start = ((), (), s32[]{:S(2)}) async-start(), calls=%async_computation.4 | async-start | bytes 4456448 | tf_op jit(solution)/shard_map/all_gather | solution.py:85
  8.7 210.1 %all-gather.9.cloned.1.call-start = ((), (), s32[]{:S(2)}) async-start(), calls=%async_computation.5 | async-start | bytes 5570560 | tf_op jit(solution)/shard_map/all_gather | solution.py:96
  13.1 1.3 copy-start.7
  151.4 2.8 copy-start.3
  154.3 7.1 %copy-start.4 = (f32[2,32,4,5,32]{1,4,3,2,0:T(8,128)S(1)}, f32[2,32,4,5,32]{1,4,3,2,0:T(8,128)}, u32[]{:S(2)}) copy-start(f32[2,32,4,5,32]{1,4,3,2,0:T(8,128)} %get-tuple-element.24) | copy-start | bytes 491524
  163.0 60.8 %copy-start.11 = (s32[2,32]{1,0:T(2,128)S(1)}, s32[2,32]{1,0:T(2,128)}, u32[]{:S(2)}) copy-start(s32[2,32]{1,0:T(2,128)} %param.23) | copy-start | bytes 772
  163.0 60.9 %copy-start.12 = (u32[32]{0:T(128)S(1)}, u32[32]{0:T(128)}, u32[]{:S(2)}) copy-start(u32[32]{0:T(128)} %constant.58) | copy-start | bytes 388
  163.0 63.1 %copy-start.9 = (f32[2]{0:T(128)S(1)}, f32[2]{0:T(128)}, u32[]{:S(2)}) copy-start(f32[2]{0:T(128)} %param.27) | copy-start | bytes 28
  163.0 102.8 %copy-start.5 = (s32[32]{0:T(128)S(1)}, s32[32]{0:T(128)}, u32[]{:S(2)}) copy-start(s32[32]{0:T(128)} %param.26) | copy-start | bytes 388
  163.0 102.8 %copy-start.8 = (s32[2]{0:T(128)S(1)}, s32[2]{0:T(128)}, u32[]{:S(2)}) copy-start(s32[2]{0:T(128)} %copy-done.7) | copy-start | bytes 28
  164.3 117.8 %copy-start.10 = (f32[2560]{0:T(1024)S(1)}, f32[2560]{0:T(1024)}, u32[]{:S(2)}) copy-start(f32[2560]{0:T(1024)} %param.21) | copy-start | bytes 30724
  164.3 114.1 %all-gather.11.cloned.1.call-start = ((), (), s32[]{:S(2)}) async-start(), calls=%async_computation.6 | async-start | bytes 5570560 | tf_op jit(solution)/shard_map/all_gather | solution.py:103
  278.4 4.0 %copy-start.2 = (bf16[1024,2560]{0,1:T(8,128)(2,1)S(1)}, bf16[1024,2560]{0,1:T(8,128)(2,1)}, u32[]{:S(2)}) copy-start(bf16[1024,2560]{0,1:T(8,128)(2,1)} %all-gather.11.cloned.1.call-done) | copy-start | bytes 15728644
  314.0 13.8 %all-to-all-start.1 = ((f32[1,16,64]{2,0,1:T(1,128)}), f32[1,16,64]{2,0,1:T(1,128)S(1)}, u32[]{:S(2)}, u32[]{:S(2)}) async-start(f32[1,16,64]{2,0,1:T(1,128)} %all_to_all.36), calls=%async_computation.1 | async-start | bytes 16384 | tf_op jit(solution)/shard_map/all_to_all | solution.py:108
  317.5 33.9 %copy-start.1 = (bf16[2560,160]{0,1:T(8,128)(2,1)S(1)}, bf16[2560,160]{0,1:T(8,128)(2,1)}, u32[]{:S(2)}) copy-start(bf16[2560,160]{0,1:T(8,128)(2,1)} %param.20) | copy-start | bytes 2457604
  317.5 32.6 %copy-start.6 = (s32[2]{0:T(128)S(1)}, s32[2]{0:T(128)}, u32[]{:S(2)}) copy-start(s32[2]{0:T(128)} %param.24) | copy-start | bytes 28
  327.8 12.4 %all-to-all-start.2 = ((f32[1,16,64]{2,0,1:T(1,128)}), f32[1,16,64]{2,0,1:T(1,128)S(1)}, u32[]{:S(2)}, u32[]{:S(2)}) async-start(f32[1,16,64]{2,0,1:T(1,128)} %all_to_all.38), calls=%async_computation.2 | async-start | bytes 16384 | tf_op jit(solution)/shard_map/all_to_all | solution.py:109
  340.2 9.8 %all-to-all-start = ((f32[1,16,64]{2,0,1:T(1,128)}), f32[1,16,64]{2,0,1:T(1,128)S(1)}, u32[]{:S(2)}, u32[]{:S(2)}) async-start(f32[1,16,64]{2,0,1:T(1,128)} %all_to_all.34), calls=%async_computation | async-start | bytes 16384 | tf_op jit(solution)/shard_map/all_to_all | solution.py:110
Sparse Core Ops, SparseCore 0:
  10.2 53.1 all-gather.4
  65.5 48.9 all-gather.6
  164.4 54.2 all-gather.8
  223.9 54.4 all-gather.10
where the time goes:
time: 359 us; the launch traced here: 358 us
  waiting for transfers between devices  168 us (47%)
  matrix products  51 us (14%)
  local copies, waits for them, and re-layouts  45.2 us (13%)
  blocking collectives  39.5 us (11%)
  other arithmetic  25.7 us (7%)
  between operations  15.3 us (4%)
  starting transfers between devices  13.2 us (4%)
    all_gather x1, waiting for transfers between devices, per_device(): lax.all_gather(attended, 'seq', axis=0, tiled=True)  54.1 us
    all_gather x1, waiting for transfers between devices, per_device(): lax.all_gather(prefix_key, 'seq', axis=1, tiled=True)  47.4 us
    all_gather x1, waiting for transfers between devices, per_device(): lax.all_gather(prefix_value, 'seq', axis=1, tiled=True)  40.7 us
    unnamed x2, blocking collectives  39.5 us
    dot_general x1, matrix products, shard_stats(): logits = jnp.dot(normed, head, preferred_element_type=jnp.float32)  30.9 us
    all_gather x1, waiting for transfers between devices, per_device(): whole = lax.all_gather(hidden_cols, 'seq', axis=1, tiled=True)  12.4 us
    gather x3, local copies, waits for them, and re-layouts, per_device(): jnp.take(lax.all_gather(prefix_value, 'seq', axis=1, tiled=True), own_gro...  11.7 us
    gather x3, local copies, waits for them, and re-layouts, per_device(): jnp.take(lax.all_gather(prefix_key, 'seq', axis=1, tiled=True), own_group...  10.5 us
  transfers between devices with their start and end apart: 7, of which 6 were waited for; matrix products, arithmetic and copies ran while one was open for 8% of the time, Pallas kernels for 0%

commit v1 on v0

v1 whole, which is shorter than its diff:
```python
import functools

import jax
import jax.numpy as jnp
from jax import lax
from jax.experimental import pallas as pl
from jax.experimental.pallas import tpu as pltpu
from jax.sharding import PartitionSpec as P

HD = 128
GROUP = 16
NEGATIVE = -1e30
EPSILON = 1e-06
REWARD_FLOOR = 0.25
MESH = pl.DeviceIdType.MESH
VMEM = pltpu.VMEM
LIMIT = 60 * 1024 * 1024


class Place:
    def __init__(self, n, planes):
        self.n, self.planes = n, planes
        self.lanes = n // planes
        self.half = self.lanes // 2
        self.me = lax.axis_index("seq")
        self.plane = self.me // self.lanes
        lane = self.me % self.lanes
        self.row = lane // 2
        self.core = lane % 2

    def device(self, plane, row, core):
        return plane * self.lanes + row * 2 + core

    def plane_at(self, step):
        return (self.plane + step) % self.planes

    def row_at(self, step):
        return (self.row + step) % self.half

    def peers(self):
        out = [self.device(self.plane_at(d), self.row, self.core) for d in range(1, self.planes)]
        out += [self.device(self.plane, self.row_at(e), self.core) for e in range(1, self.half)]
        return out + [self.device(self.plane, self.row, 1 - self.core)]


def greet(peers):
    barrier = pltpu.get_barrier_semaphore()
    for peer in peers:
        pl.semaphore_signal(barrier, inc=1, device_id={"seq": peer}, device_id_type=MESH)
    pl.semaphore_wait(barrier, len(peers))


def send_count(n, planes):
    half = n // planes // 2
    return (planes - 1) + half + (planes - 1) * half + planes * (half - 1)


class Spread:
    def __init__(self, at, parts, own, full, send_sem, recv_sem, local_sem):
        self.at, self.parts, self.own, self.full = at, parts, own, full
        self.send_sem, self.recv_sem, self.local_sem = send_sem, recv_sem, local_sem
        self.sent = []

    def send(self, src_ref, source, part, target):
        copy = pltpu.make_async_remote_copy(
            src_ref=src_ref,
            dst_ref=self.full(source, part),
            send_sem=self.send_sem.at[len(self.sent)],
            recv_sem=self.recv_sem.at[source * self.parts + part],
            device_id={"seq": target},
            device_id_type=MESH,
        )
        copy.start()
        self.sent.append(copy)

    def arrived(self, source, part):
        pltpu.make_async_remote_copy(
            src_ref=self.full(source, part),
            dst_ref=self.full(source, part),
            send_sem=self.send_sem.at[0],
            recv_sem=self.recv_sem.at[source * self.parts + part],
            device_id={"seq": self.at.device(self.at.plane, self.at.row, 1 - self.at.core)},
            device_id_type=MESH,
        ).wait_recv()

    def to_rows(self, src_ref, source, part):
        at = self.at
        for e in range(1, at.half):
            self.send(src_ref, source, part, at.device(at.plane, at.row_at(e), at.core))

    def to_core(self, src_ref, source, part):
        at = self.at
        self.send(src_ref, source, part, at.device(at.plane, at.row, 1 - at.core))

    def start(self):
        at = self.at
        self.local = []
        for part in range(self.parts):
            for d in range(1, at.planes):
                target = at.plane_at(d)
                self.send(
                    self.own(part, target), at.me, part, at.device(target, at.row, at.core)
                )
            self.to_rows(self.own(part, at.plane), at.me, part)
            self.to_core(self.own(part, at.plane), at.me, part)
            copy = pltpu.make_async_copy(
                self.own(part, at.plane), self.full(at.me, part), self.local_sem.at[part]
            )
            copy.start()
            self.local.append(copy)

    def from_rows(self, plane):
        at = self.at
        for part in range(self.parts):
            for e in range(1, at.half):
                source = at.device(plane, at.row_at(e), at.core)
                self.arrived(source, part)
                self.to_core(self.full(source, part), source, part)

    def from_plane(self, plane):
        at = self.at
        for part in range(self.parts):
            source = at.device(plane, at.row, at.core)
            self.arrived(source, part)
            self.to_rows(self.full(source, part), source, part)
            self.to_core(self.full(source, part), source, part)

    def finish(self):
        at = self.at
        order = [at.plane_at(d) for d in [1, at.planes - 1] + list(range(2, at.planes - 1))]
        self.from_rows(at.plane)
        for i, plane in enumerate(order):
            self.from_plane(plane)
            if i >= 1:
                self.from_rows(order[i - 1])
        self.from_rows(order[-1])
        for plane in range(at.planes):
            for row in range(at.half):
                for part in range(self.parts):
                    self.arrived(at.device(plane, row, 1 - at.core), part)
        for copy in self.sent:
            copy.wait_send()
        for copy in self.local:
            copy.wait()


def exchange_kernel(
    n,
    planes,
    q_ref,
    ck_ref,
    cv_ref,
    pk_ref,
    pv_ref,
    meta_ref,
    q_out,
    ck_out,
    cv_out,
    pk_out,
    pv_out,
    meta_out,
    send_sem,
    recv_sem,
    local_sem,
    lane_send,
    lane_recv,
    lane_local,
    meta_send,
    meta_recv,
    meta_local,
):
    at = Place(n, planes)
    greet([(at.me + d) % n for d in range(1, n)])
    conts = q_ref.shape[0]
    span = pk_ref.shape[1]

    def head(ref, plane):
        width = ref.shape[2] // planes
        return ref.at[:, :, pl.ds(pl.multiple_of(plane * width, 128), width)]

    def own(part, plane):
        return head((pk_ref, pv_ref)[part], plane)

    def full(source, part):
        start = pl.multiple_of(source * span, 128)
        return (pk_out, pv_out)[part].at[:, pl.ds(start, span), :]

    spread = Spread(at, 2, own, full, send_sem, recv_sem, local_sem)
    spread.start()
    pairs = ((q_ref, q_out), (ck_ref, ck_out), (cv_ref, cv_out))
    waits = []
    for i, (src, dst) in enumerate(pairs):
        mine = dst.at[pl.ds(at.plane * conts, conts)]
        for d in range(1, planes):
            target = at.plane_at(d)
            copy = pltpu.make_async_remote_copy(
                src_ref=head(src, target),
                dst_ref=mine,
                send_sem=lane_send.at[i * planes + d],
                recv_sem=lane_recv.at[i * planes + at.plane],
                device_id={"seq": at.device(target, at.row, at.core)},
                device_id_type=MESH,
            )
            copy.start()
            waits.append(copy.wait_send)
        copy = pltpu.make_async_copy(head(src, at.plane), mine, lane_local.at[i])
        copy.start()
        waits.append(copy.wait)
    for d in range(1, n):
        copy = pltpu.make_async_remote_copy(
            src_ref=meta_ref,
            dst_ref=meta_out.at[at.me],
            send_sem=meta_send.at[d],
            recv_sem=meta_recv.at[at.me],
            device_id={"seq": (at.me + d) % n},
            device_id_type=MESH,
        )
        copy.start()
        waits.append(copy.wait_send)
    copy = pltpu.make_async_copy(meta_ref, meta_out.at[at.me], meta_local)
    copy.start()
    waits.append(copy.wait)
    spread.finish()
    for i, (src, dst) in enumerate(pairs):
        for d in range(1, planes):
            source = at.plane_at(d)
            landed = dst.at[pl.ds(source * conts, conts)]
            pltpu.make_async_remote_copy(
                src_ref=landed,
                dst_ref=landed,
                send_sem=lane_send.at[i * planes + d],
                recv_sem=lane_recv.at[i * planes + source],
                device_id={"seq": at.device(source, at.row, at.core)},
                device_id_type=MESH,
            ).wait_recv()
    for d in range(1, n):
        source = (at.me + d) % n
        pltpu.make_async_remote_copy(
            src_ref=meta_ref,
            dst_ref=meta_out.at[source],
            send_sem=meta_send.at[d],
            recv_sem=meta_recv.at[source],
            device_id={"seq": source},
            device_id_type=MESH,
        ).wait_recv()
    for wait in waits:
        wait()


def exchange(n, planes, q, ck, cv, pk, pv, meta):
    conts, steps, width = q.shape
    prompts, span, _ = pk.shape
    dma = pltpu.SemaphoreType.DMA
    shape = jax.ShapeDtypeStruct
    return pl.pallas_call(
        functools.partial(exchange_kernel, n, planes),
        out_shape=(
            shape((conts * planes, steps, width // planes), q.dtype),
            shape((conts * planes, steps, ck.shape[2] // planes), q.dtype),
            shape((conts * planes, steps, ck.shape[2] // planes), q.dtype),
            shape((prompts, span * n, pk.shape[2] // planes), q.dtype),
            shape((prompts, span * n, pk.shape[2] // planes), q.dtype),
            shape((n,) + meta.shape, meta.dtype),
        ),
        in_specs=[pl.BlockSpec(memory_space=VMEM)] * 6,
        out_specs=(pl.BlockSpec(memory_space=VMEM),) * 6,
        scratch_shapes=[
            dma((2 * send_count(n, planes),)),
            dma((2 * n,)),
            dma((2,)),
            dma((3 * planes,)),
            dma((3 * planes,)),
            dma((3,)),
            dma((n,)),
            dma((n,)),
            dma,
        ],
        compiler_params=pltpu.CompilerParams(
            collective_id=0, has_side_effects=True, vmem_limit_bytes=LIMIT
        ),
        name="exchange",
    )(q, ck, cv, pk, pv, meta)


def attention_kernel(group_ref, length_ref, q_ref, ck_ref, cv_ref, pk_ref, pv_ref, out_ref):
    cont = pl.program_id(0)
    prompt = group_ref[cont]
    length = length_ref[prompt]
    steps, width = q_ref.shape[1:]
    heads = width // HD
    q = q_ref[0]
    rows = jnp.concatenate([q[:, h * HD : (h + 1) * HD] for h in range(heads)], axis=0)
    contract = (((1,), (1,)), ((), ()))
    early = lax.dot_general(rows, pk_ref[prompt], contract, preferred_element_type=jnp.float32)
    late = lax.dot_general(rows, ck_ref[0], contract, preferred_element_type=jnp.float32)
    scale = HD ** (-0.5)
    column = lax.broadcasted_iota(jnp.int32, early.shape, 1)
    early = jnp.where(column < length, early * scale, NEGATIVE)
    line = lax.broadcasted_iota(jnp.int32, late.shape, 0) % steps
    late = jnp.where(
        lax.broadcasted_iota(jnp.int32, late.shape, 1) <= line, late * scale, NEGATIVE
    )
    peak = jnp.maximum(
        jnp.max(early, axis=1, keepdims=True), jnp.max(late, axis=1, keepdims=True)
    )
    early = jnp.exp(early - peak).astype(jnp.bfloat16)
    late = jnp.exp(late - peak).astype(jnp.bfloat16)
    total = jnp.sum(early.astype(jnp.float32), axis=1, keepdims=True) + jnp.sum(
        late.astype(jnp.float32), axis=1, keepdims=True
    )
    mixed = jnp.dot(early, pv_ref[prompt], preferred_element_type=jnp.float32) + jnp.dot(
        late, cv_ref[0], preferred_element_type=jnp.float32
    )
    mixed = (mixed / total).astype(jnp.bfloat16)
    out_ref[...] = jnp.concatenate(
        [mixed[h * steps : (h + 1) * steps] for h in range(heads)], axis=1
    )


def attention(groups, lengths, q, ck, cv, pk, pv):
    conts, steps, width = q.shape
    whole = pl.BlockSpec(memory_space=VMEM)
    scalar = pl.BlockSpec(memory_space=pltpu.SMEM)
    return pl.pallas_call(
        attention_kernel,
        out_shape=jax.ShapeDtypeStruct((conts * steps, width), jnp.bfloat16),
        grid=(conts,),
        in_specs=[
            scalar,
            scalar,
            pl.BlockSpec((1, steps, width), lambda c: (c, 0, 0)),
            pl.BlockSpec((1, steps, ck.shape[2]), lambda c: (c, 0, 0)),
            pl.BlockSpec((1, steps, ck.shape[2]), lambda c: (c, 0, 0)),
            whole,
            whole,
        ],
        out_specs=pl.BlockSpec((steps, width), lambda c: (c, 0)),
        compiler_params=pltpu.CompilerParams(vmem_limit_bytes=LIMIT),
        name="attention",
    )(groups, lengths, q, ck, cv, pk, pv)


PARTS = 2


def tokens_kernel(n, planes, x_ref, out_ref, send_sem, recv_sem, local_sem):
    at = Place(n, planes)
    greet(at.peers())
    rows, width = x_ref.shape
    piece = rows // PARTS

    def own(part, plane):
        return x_ref.at[pl.ds(part * piece, piece)]

    def full(source, part):
        start = pl.multiple_of(source % at.lanes * rows + part * piece, 16)
        column = pl.multiple_of(source // at.lanes * width, 128)
        return out_ref.at[pl.ds(start, piece), pl.ds(column, width)]

    spread = Spread(at, PARTS, own, full, send_sem, recv_sem, local_sem)
    spread.start()
    spread.finish()


def features_kernel(n, planes, x_ref, out_ref, send_sem, recv_sem, local_sem):
    at = Place(n, planes)
    greet(at.peers())
    rows, width = x_ref.shape
    piece = width // PARTS

    def own(part, plane):
        return x_ref.at[:, pl.ds(part * piece, piece)]

    def full(source, part):
        start = pl.multiple_of(source * rows, 16)
        return out_ref.at[pl.ds(start, rows), pl.ds(part * piece, piece)]

    spread = Spread(at, PARTS, own, full, send_sem, recv_sem, local_sem)
    spread.start()
    spread.finish()


def gather(kernel, n, planes, x, shape, number, name):
    dma = pltpu.SemaphoreType.DMA
    return pl.pallas_call(
        functools.partial(kernel, n, planes),
        out_shape=jax.ShapeDtypeStruct(shape, x.dtype),
        in_specs=[pl.BlockSpec(memory_space=VMEM)],
        out_specs=pl.BlockSpec(memory_space=VMEM),
        scratch_shapes=[
            dma((PARTS * send_count(n, planes),)),
            dma((PARTS * n,)),
            dma((PARTS,)),
        ],
        compiler_params=pltpu.CompilerParams(
            collective_id=number, has_side_effects=True, vmem_limit_bytes=LIMIT
        ),
        name=name,
    )(x)


TILE = 256


def logits_kernel(vocab, offset_ref, x_ref, ids_ref, head_ref, max_ref, sum_ref, pick_ref):
    step = pl.program_id(0)

    @pl.when(step == 0)
    def _():
        max_ref[...] = jnp.full_like(max_ref, NEGATIVE)
        sum_ref[...] = jnp.zeros_like(sum_ref)
        pick_ref[...] = jnp.zeros_like(pick_ref)

    logits = jnp.dot(x_ref[...], head_ref[...], preferred_element_type=jnp.float32)
    column = step * TILE + lax.broadcasted_iota(jnp.int32, (1, TILE), 1)
    wanted = ids_ref[...] - offset_ref[0]
    wanted = jnp.where(wanted < vocab, wanted, -1)
    logits = jnp.where(column < vocab, logits, NEGATIVE)
    best = max_ref[...]
    for at in range(0, TILE, 128):
        best = jnp.maximum(best, logits[:, at : at + 128])
    mass = sum_ref[...] * jnp.exp(max_ref[...] - best)
    pick = pick_ref[...]
    for at in range(0, TILE, 128):
        mass += jnp.exp(logits[:, at : at + 128] - best)
        pick += jnp.where(column[:, at : at + 128] == wanted, logits[:, at : at + 128], 0.0)
    max_ref[...] = best
    sum_ref[...] = mass
    pick_ref[...] = pick


def logit_stats(x, ids, head, offset):
    rows, depth = x.shape
    vocab = head.shape[1]
    whole = pl.BlockSpec((rows, 128), lambda v: (0, 0))
    return pl.pallas_call(
        functools.partial(logits_kernel, vocab),
        out_shape=(jax.ShapeDtypeStruct((rows, 128), jnp.float32),) * 3,
        grid=(pl.cdiv(vocab, TILE),),
        in_specs=[
            pl.BlockSpec(memory_space=pltpu.SMEM),
            pl.BlockSpec(memory_space=VMEM),
            pl.BlockSpec(memory_space=VMEM),
            pl.BlockSpec((depth, TILE), lambda v: (0, v)),
        ],
        out_specs=(whole,) * 3,
        compiler_params=pltpu.CompilerParams(vmem_limit_bytes=LIMIT),
        name="logits",
    )(offset, x, ids, head)


def stats_kernel(n, x_ref, out_ref, send_sem, recv_sem, local_sem):
    me = lax.axis_index("seq")
    greet([(me + d) % n for d in range(1, n)])
    sent = []
    for d in range(1, n):
        target = (me + d) % n
        copy = pltpu.make_async_remote_copy(
            src_ref=x_ref.at[target],
            dst_ref=out_ref.at[me],
            send_sem=send_sem.at[d],
            recv_sem=recv_sem.at[me],
            device_id={"seq": target},
            device_id_type=MESH,
        )
        copy.start()
        sent.append(copy)
    local = pltpu.make_async_copy(x_ref.at[me], out_ref.at[me], local_sem)
    local.start()
    for d in range(1, n):
        source = (me + d) % n
        pltpu.make_async_remote_copy(
            src_ref=x_ref.at[source],
            dst_ref=out_ref.at[source],
            send_sem=send_sem.at[d],
            recv_sem=recv_sem.at[source],
            device_id={"seq": source},
            device_id_type=MESH,
        ).wait_recv()
    for copy in sent:
        copy.wait_send()
    local.wait()


def stats_exchange(n, x):
    dma = pltpu.SemaphoreType.DMA
    return pl.pallas_call(
        functools.partial(stats_kernel, n),
        out_shape=jax.ShapeDtypeStruct(x.shape, x.dtype),
        in_specs=[pl.BlockSpec(memory_space=VMEM)],
        out_specs=pl.BlockSpec(memory_space=VMEM),
        scratch_shapes=[dma((n,)), dma((n,)), dma],
        compiler_params=pltpu.CompilerParams(collective_id=3, has_side_effects=True),
        name="stats",
    )(x)


def per_device(
    n,
    cont_query,
    cont_key,
    cont_value,
    prefix_key,
    prefix_value,
    out_weight,
    norm_gain,
    lm_head,
    target_ids,
    cont_len,
    prompt_len,
    group_of,
    rewards,
):
    cont_count, cont_span, query_width = cont_query.shape
    own_rows = cont_count * cont_span
    planes = cont_key.shape[2] // HD
    lanes = n // planes
    total_rows = own_rows * n
    device_index = lax.axis_index("seq")
    lane = device_index % lanes

    meta = jnp.zeros((8, 128), jnp.float32)
    meta = meta.at[0, :own_rows].set(target_ids.reshape(own_rows).astype(jnp.float32))
    meta = meta.at[1, :cont_count].set(rewards)
    q, ck, cv, pk, pv, meta = exchange(
        n, planes, cont_query, cont_key, cont_value, prefix_key, prefix_value, meta
    )

    def by_lane(x):
        return jnp.swapaxes(x.reshape((planes, lanes) + x.shape[1:]), 0, 1)

    lane_groups = lax.dynamic_index_in_dim(
        by_lane(group_of.reshape(n, cont_count)), lane, 0, keepdims=False
    ).reshape(planes * cont_count)
    attended = attention(lane_groups, prompt_len, q, ck, cv, pk, pv)
    tokens = gather(
        tokens_kernel, n, planes, attended, (total_rows, query_width), 1, "tokens"
    )
    hidden_cols = lax.dot_general(
        out_weight, tokens, (((0,), (1,)), ((), ())), preferred_element_type=jnp.float32
    ).astype(jnp.bfloat16)
    whole = gather(
        features_kernel, n, planes, hidden_cols, (out_weight.shape[0], total_rows), 2, "features"
    )
    widened = whole.astype(jnp.float32)
    factor = lax.rsqrt(jnp.mean(widened * widened, axis=0, keepdims=True) + EPSILON)
    normed = (widened * factor * norm_gain[:, None]).astype(jnp.bfloat16).T

    ids = by_lane(meta[:, 0, :own_rows]).reshape(total_rows, 1).astype(jnp.int32)
    offset = (device_index * lm_head.shape[1]).astype(jnp.int32).reshape(1)
    peak, mass, pick = logit_stats(normed, ids, lm_head, offset)
    top = jnp.max(peak, axis=1)
    mass = jnp.sum(mass * jnp.exp(peak - top[:, None]), axis=1)
    pick = jnp.sum(pick, axis=1)
    stacked = jnp.stack([top, mass, pick]).reshape(3, lanes, planes, own_rows)
    stacked = stacked.transpose(2, 1, 0, 3).reshape(n, 3, own_rows)
    stacked = jnp.pad(stacked, ((0, 0), (0, 5), (0, 128 - own_rows)))
    shares = stats_exchange(n, stacked)[:, :3, :own_rows]
    maximum = jnp.max(shares[:, 0], axis=0)
    total_mass = jnp.sum(shares[:, 1] * jnp.exp(shares[:, 0] - maximum[None, :]), axis=0)
    picked = jnp.sum(shares[:, 2], axis=0)
    logprob = (picked - maximum - jnp.log(total_mass)).reshape(cont_count, cont_span)
    position = jnp.arange(cont_span, dtype=jnp.int32)
    live = position[None, :] < cont_len[:, None]
    token_logprob = jnp.where(live, logprob, 0.0)

    every_reward = meta[:, 1, :cont_count].reshape(n * cont_count)
    own_groups = lax.dynamic_slice_in_dim(group_of, device_index * cont_count, cont_count)
    same = (own_groups[:, None] == group_of[None, :]).astype(jnp.float32)
    group_mean = jnp.sum(same * every_reward[None, :], axis=1) / GROUP
    deviation = every_reward[None, :] - group_mean[:, None]
    spread = jnp.sqrt(jnp.sum(same * deviation * deviation, axis=1) / (GROUP - 1))
    advantage = (rewards - group_mean) / jnp.maximum(spread, REWARD_FLOOR)
    objective = advantage * jnp.sum(token_logprob, axis=1) / cont_len.astype(jnp.float32)
    return (token_logprob, advantage, objective)


def solution(mesh):
    placed = (
        P(("grp", "seq"), None, None),
        P(("grp", "seq"), None, None),
        P(("grp", "seq"), None, None),
        P("grp", "seq", None),
        P("grp", "seq", None),
        P(None, "seq"),
        P(),
        P(None, "seq"),
        P(("grp", "seq"), None),
        P(("grp", "seq")),
        P("grp"),
        P("grp"),
        P(("grp", "seq")),
    )
    return jax.shard_map(
        functools.partial(per_device, mesh.shape["seq"]),
        mesh=mesh,
        in_specs=placed,
        out_specs=(P(("grp", "seq"), None), P(("grp", "seq")), P(("grp", "seq"))),
        check_vma=False,
    )
```

time: 359 us -> 271 us (0.75)
  Pallas kernels: 0 us -> 202 us
  waiting for transfers between devices: 168 us -> 0 us
  matrix products: 51 us -> 5.05 us
  blocking collectives: 39.5 us -> 0 us
  between operations: 15.3 us -> 0.79 us
  starting transfers between devices: 13.2 us -> 0 us
  other arithmetic: 25.7 us -> 16.1 us
    pallas_call x0 -> x6, Pallas kernels: none -> 202 us  [the longest x2 104 us: gather(): pl.pallas_call(functools.partial(kernel, n, planes), out_shape=jax.ShapeD...]
    all_gather x4 -> x0, waiting for transfers between devices: 155 us -> none  [the longest x1 54.1 us: per_device(): lax.all_gather(attended, 'seq', axis=0, tiled=True)]
    dot_general x7 -> x1, matrix products: 51 us -> 5.05 us  [per_device(): lax.dot_general(out_weight, tokens, (((0,), (1,)), ((), ())), preferred_e...]
    unnamed x2 -> x0, blocking collectives: 39.5 us -> none
    unnamed x31 -> x17, local copies, waits for them, and re-layouts: 1.38 us -> 31.7 us
    gather x7 -> x0, local copies, waits for them, and re-layouts: 23.4 us -> none  [the longest x3 11.7 us: per_device(): jnp.take(lax.all_gather(prefix_value, 'seq', axis=1, tiled=True), own_gro...]
    reshape x7 -> x1, local copies, waits for them, and re-layouts: 18.1 us -> 0.6 us  [per_device(): lane_groups = lax.dynamic_index_in_dim(by_lane(group_of.reshape(n, cont_c...]
    all_to_all x3 -> x0, starting transfers between devices: 12.9 us -> none  [the longest x1 5.97 us: per_device(): lax.all_to_all(total_mass[None, :], 'seq', split_axis=1, concat_axis=0, t...]
  transfers between devices with their start and end apart: 7 -> 0, of which waited for: 6 -> 0; matrix products, arithmetic and copies ran while one was open for 8% -> 0% of each run, Pallas kernels for 0% -> 0%
where the time goes in v1:
time: 271 us; the launch traced here: 270 us
  Pallas kernels  202 us (75%)
  local copies, waits for them, and re-layouts  45.6 us (17%)
  other arithmetic  16.1 us (6%)
  matrix products  5.05 us (2%)
    pallas_call x2, Pallas kernels, gather(): pl.pallas_call(functools.partial(kernel, n, planes), out_shape=jax.ShapeD...  104 us
    pallas_call x1, Pallas kernels, logit_stats(): pl.pallas_call(functools.partial(logits_kernel, vocab), out_shape=(jax.Sh...  36.7 us
    pallas_call x1, Pallas kernels, exchange(): pl.pallas_call(functools.partial(exchange_kernel, n, planes), out_shape=(...  33.4 us
    unnamed x17, local copies, waits for them, and re-layouts  31.7 us
    pallas_call x1, Pallas kernels, stats_exchange(): pl.pallas_call(functools.partial(stats_kernel, n), out_shape=jax.ShapeDty...  17.4 us
    pallas_call x1, Pallas kernels, attention(): pl.pallas_call(attention_kernel, out_shape=jax.ShapeDtypeStruct((conts *...  10.2 us
    pallas_call x1, local copies, waits for them, and re-layouts, gather(): pl.pallas_call(functools.partial(kernel, n, planes), out_shape=jax.ShapeD...  7.72 us

profile of v1, /device:TPU:0, one launch (start us, length us, event | category | flops | bytes accessed | tf_op | source)
XLA Modules:
  0.0 269.7 jit_solution(566513710188455263)
XLA Ops:
  0.6 0.0 copy-start
  0.7 0.8 dynamic_slice.5
  1.5 0.7 convert_element_type.37
  2.2 0.1 convert_element_type.38
  2.2 0.7 scatter.9.meta_ref
  3.0 0.0 copy-start.3
  3.0 0.7 reshape_reshape.3
  3.8 0.6 reshape.132.group_ref
  4.4 0.0 copy-done.3
  4.4 33.4 %exchange.1 = (bf16[8,32,640]{2,1,0:T(8,128)(2,1)}, bf16[8,32,128]{2,1,0:T(8,128)(2,1)}, bf16[8,32,128]{2,1,0:T(8,128)(2,1)}, bf16[2,2048,128]{2,1,0:T(8,128)(2,...) custom-call(bf16[2,32,2560]{2,1,0:T(8,128)(2,1)} %q_ref.1, bf16[2,32,512]{2,1,0:T(8,128)(2,1)} %ck_ref.1, ...), custom_call_target="tpu_custom_call" | custom-call | tf_op jit(solution)/shard_map/exchange/pallas_call | solution.py:255
  37.8 10.2 %attention.1.x_ref = bf16[256,640]{1,0:T(8,128)(2,1)} custom-call(s32[8]{0:T(128)} %reshape.132.group_ref, s32[2]{0:T(128)} %length_ref.1, bf16[8,32,640]{2,1,0:T(8,128)(2,1)} %get-tuple-element.36.q_ref, bf16[8,32,128]{2,1,0:T(8,128)(2,1)} %get-tuple-element.37.ck_ref, bf16[8,32,128]{2,1,0:T(8,128)(2,1)} %get-tuple-element.38.cv_ref, ...), custom_call_target="tpu_custom_call" | custom-call | tf_op jit(solution)/shard_map/attention/pallas_call | solution.py:324
  48.1 0.9 slice_reduce_fusion
  48.9 0.8 slice_convert_fusion
  49.8 0.1 mul.59
  49.9 0.8 fusion.7
  50.7 1.3 convert_element_type.48.ids_ref
  52.0 48.4 %tokens.1 = bf16[1024,2560]{1,0:T(8,128)(2,1)} custom-call(bf16[256,640]{1,0:T(8,128)(2,1)} %attention.1.x_ref), custom_call_target="tpu_custom_call" | custom-call | tf_op jit(solution)/shard_map/tokens/pallas_call | solution.py:385
  100.4 0.0 copy-done
  100.4 5.1 %fusion.4.x_ref = bf16[160,1024]{1,0:T(8,128)(2,1)} fusion(bf16[1024,2560]{1,0:T(8,128)(2,1)} %tokens.1, bf16[2560,160]{0,1:T(8,128)(2,1)S(1)} %copy-done), kind=kOutput, calls=%fused_computation.7 | convolution fusion | flops 839024640 | bytes 6389760 | tf_op jit(solution)/shard_map/dot_general | solution.py:539
  105.5 56.0 %features.1 = bf16[2560,1024]{1,0:T(8,128)(2,1)} custom-call(bf16[160,1024]{1,0:T(8,128)(2,1)} %fusion.4.x_ref), custom_call_target="tpu_custom_call" | custom-call | tf_op jit(solution)/shard_map/features/pallas_call | solution.py:385
  161.5 7.7 %copy.20 = bf16[2560,1024]{0,1:T(8,128)(2,1)} copy(bf16[2560,1024]{1,0:T(8,128)(2,1)} %features.1) | data formatting | bytes 10485760 | tf_op jit(solution)/shard_map/features/pallas_call | solution.py:385
  169.2 0.0 copy-start.2
  169.2 0.0 copy-start.4
  169.2 3.7 %fusion = f32[1024]{0:T(1024)S(1)} fusion(bf16[2560,1024]{0,1:T(8,128)(2,1)} %copy.20), kind=kLoop, calls=%fused_computation.2 | loop fusion | flops 7863296 | bytes 5246976 | tf_op jit(solution)/shard_map/reduce_sum | solution.py:546
  172.9 0.3 copy-done.2
  173.2 0.0 copy-done.4
  173.2 3.6 %fusion.3.x_ref = bf16[1024,2560]{1,0:T(8,128)(2,1)} fusion(bf16[2560,1024]{0,1:T(8,128)(2,1)S(1)} %copy-done.2, f32[2560]{0:T(1024)S(1)} %copy-done.4, f32[1024]{0:T(1024)S(1)} %add_rsqrt_fusion), kind=kLoop, calls=%fused_computation.5 | loop fusion | flops 10485760 | bytes 10500096 | tf_op jit(solution)/shard_map/transpose | solution.py:547
  176.9 31.3 %copy.23.head_ref = bf16[2560,4752]{1,0:T(8,128)(2,1)} copy(bf16[2560,4752]{0,1:T(8,128)(2,1)} %param.24) | data formatting | bytes 48660480 | tf_op args[7]
  208.2 0.0 copy-start.5
  208.2 0.0 copy-start.7
  208.2 0.0 copy-start.6
  208.2 0.0 copy-start.1
  208.2 36.7 %logits.1 = (f32[1024,128]{1,0:T(8,128)}, f32[1024,128]{1,0:T(8,128)}, f32[1024,128]{1,0:T(8,128)}) custom-call(s32[1]{0:T(128)} %bitcast.offset_ref, bf16[1024,2560]{1,0:T(8,128)(2,1)} %fusion.3.x_ref, s32[1024,1]{1,0:T(8,128)} %convert_element_type.48.ids_ref, bf16[2560,4752]{1,0:T(8,128)(2,1)} %copy.23.head_ref), custom_call_target="tpu_custom_call" | custom-call | tf_op jit(solution)/shard_map/logits/pallas_call | solution.py:436
  244.9 1.2 reduce_max.18
  246.1 1.6 multiply_reduce_fusion
  247.7 0.1 stack.12
  247.8 0.1 stack.13
  247.9 1.2 reduce_sum.74
  249.1 0.1 stack.14
  249.2 0.6 pad.12.x_ref
  249.9 17.4 %stats.1 = f32[16,8,128]{2,1,0:T(8,128)} custom-call(f32[16,8,128]{2,1,0:T(8,128)} %pad.12.x_ref), custom_call_target="tpu_custom_call" | custom-call | tf_op jit(solution)/shard_map/stats/pallas_call | solution.py:487
  267.2 1.0 slice_reduce_fusion.1
  268.3 0.1 sub.48
  268.4 0.0 copy-done.5
  268.4 0.0 copy-done.7
  268.4 0.8 fusion.8
  269.1 0.0 copy-done.6
  269.2 0.5 convert_divide_fusion
  269.7 0.0 copy-done.1
  (10 shorter events, 0.1 us)
Async XLA Ops:
  0.6 99.8 %copy-start = (bf16[2560,160]{0,1:T(8,128)(2,1)S(1)}, bf16[2560,160]{0,1:T(8,128)(2,1)}, u32[]{:S(2)}) copy-start(bf16[2560,160]{0,1:T(8,128)(2,1)} %param.22) | copy-start | bytes 2457604
  3.0 1.4 copy-start.3
  169.2 4.0 %copy-start.2 = (bf16[2560,1024]{0,1:T(8,128)(2,1)S(1)}, bf16[2560,1024]{0,1:T(8,128)(2,1)}, u32[]{:S(2)}) copy-start(bf16[2560,1024]{0,1:T(8,128)(2,1)} %copy.20) | copy-start | bytes 15728644
  169.2 4.0 %copy-start.4 = (f32[2560]{0:T(1024)S(1)}, f32[2560]{0:T(1024)}, u32[]{:S(2)}) copy-start(f32[2560]{0:T(1024)} %param.23) | copy-start | bytes 30724
  208.2 60.2 %copy-start.5 = (s32[32]{0:T(128)S(1)}, s32[32]{0:T(128)}, u32[]{:S(2)}) copy-start(s32[32]{0:T(128)} %param.28) | copy-start | bytes 388
  208.2 60.2 %copy-start.7 = (s32[2]{0:T(128)S(1)}, s32[2]{0:T(128)}, u32[]{:S(2)}) copy-start(s32[2]{0:T(128)} %param.26) | copy-start | bytes 28
  208.2 60.9 %copy-start.6 = (f32[2]{0:T(128)S(1)}, f32[2]{0:T(128)}, u32[]{:S(2)}) copy-start(f32[2]{0:T(128)} %param.29) | copy-start | bytes 28
  208.2 61.5 %copy-start.1 = (bf16[2560,160]{0,1:T(8,128)(2,1)S(1)}, bf16[2560,160]{0,1:T(8,128)(2,1)}, u32[]{:S(2)}) copy-start(bf16[2560,160]{0,1:T(8,128)(2,1)} %param.22) | copy-start | bytes 2457604

commit v2 on v1

--- a/solution.py
+++ b/solution.py
@@ -56,7 +56,8 @@
 
 
 class Spread:
-    def __init__(self, at, parts, own, full, send_sem, recv_sem, local_sem):
+    def __init__(self, at, parts, own, full, send_sem, recv_sem, local_sem, ring=True):
+        self.ring = ring
         self.at, self.parts, self.own, self.full = at, parts, own, full
         self.send_sem, self.recv_sem, self.local_sem = send_sem, recv_sem, local_sem
         self.sent = []
@@ -96,7 +97,7 @@
         at = self.at
         self.local = []
         for part in range(self.parts):
-            for d in range(1, at.planes):
+            for d in range(1, 2 if self.ring else at.planes):
                 target = at.plane_at(d)
                 self.send(
                     self.own(part, target), at.me, part, at.device(target, at.row, at.core)
@@ -117,20 +118,26 @@
                 self.arrived(source, part)
                 self.to_core(self.full(source, part), source, part)
 
-    def from_plane(self, plane):
+    def from_plane(self, plane, onward):
         at = self.at
         for part in range(self.parts):
             source = at.device(plane, at.row, at.core)
             self.arrived(source, part)
+            if onward:
+                target = at.device(at.plane_at(1), at.row, at.core)
+                self.send(self.full(source, part), source, part, target)
             self.to_rows(self.full(source, part), source, part)
             self.to_core(self.full(source, part), source, part)
 
     def finish(self):
         at = self.at
-        order = [at.plane_at(d) for d in [1, at.planes - 1] + list(range(2, at.planes - 1))]
+        steps = [1, at.planes - 1] + list(range(2, at.planes - 1))
+        if self.ring:
+            steps = list(range(at.planes - 1, 0, -1))
+        order = [at.plane_at(d) for d in steps]
         self.from_rows(at.plane)
         for i, plane in enumerate(order):
-            self.from_plane(plane)
+            self.from_plane(plane, self.ring and steps[i] > 1)
             if i >= 1:
                 self.from_rows(order[i - 1])
         self.from_rows(order[-1])
@@ -185,7 +192,7 @@
         start = pl.multiple_of(source * span, 128)
         return (pk_out, pv_out)[part].at[:, pl.ds(start, span), :]
 
-    spread = Spread(at, 2, own, full, send_sem, recv_sem, local_sem)
+    spread = Spread(at, 2, own, full, send_sem, recv_sem, local_sem, ring=False)
     spread.start()
     pairs = ((q_ref, q_out), (ck_ref, ck_out), (cv_ref, cv_out))
     waits = []
@@ -399,11 +406,16 @@
     )(x)
 
 
-TILE = 256
-
-
-def logits_kernel(vocab, offset_ref, x_ref, ids_ref, head_ref, max_ref, sum_ref, pick_ref):
+TILE = 528
+BAND = 512
+STEP = 128
+
+
+def logits_kernel(
+    vocab, offset_ref, x_ref, gain_ref, ids_ref, head_ref, max_ref, sum_ref, pick_ref, normed_ref
+):
     step = pl.program_id(0)
+    depth, tokens = x_ref.shape
 
     @pl.when(step == 0)
     def _():
@@ -411,42 +423,60 @@
         sum_ref[...] = jnp.zeros_like(sum_ref)
         pick_ref[...] = jnp.zeros_like(pick_ref)
 
-    logits = jnp.dot(x_ref[...], head_ref[...], preferred_element_type=jnp.float32)
-    column = step * TILE + lax.broadcasted_iota(jnp.int32, (1, TILE), 1)
-    wanted = ids_ref[...] - offset_ref[0]
-    wanted = jnp.where(wanted < vocab, wanted, -1)
-    logits = jnp.where(column < vocab, logits, NEGATIVE)
-    best = max_ref[...]
-    for at in range(0, TILE, 128):
-        best = jnp.maximum(best, logits[:, at : at + 128])
-    mass = sum_ref[...] * jnp.exp(max_ref[...] - best)
-    pick = pick_ref[...]
-    for at in range(0, TILE, 128):
-        mass += jnp.exp(logits[:, at : at + 128] - best)
-        pick += jnp.where(column[:, at : at + 128] == wanted, logits[:, at : at + 128], 0.0)
-    max_ref[...] = best
-    sum_ref[...] = mass
-    pick_ref[...] = pick
-
-
-def logit_stats(x, ids, head, offset):
-    rows, depth = x.shape
-    vocab = head.shape[1]
-    whole = pl.BlockSpec((rows, 128), lambda v: (0, 0))
+        def square(i, total):
+            rows = x_ref[pl.ds(pl.multiple_of(i * STEP, STEP), STEP)].astype(jnp.float32)
+            return total + jnp.sum((rows * rows).reshape(STEP // 8, 8, tokens), axis=0)
+
+        total = lax.fori_loop(0, depth // STEP, square, jnp.zeros((8, tokens), jnp.float32))
+        mean = jnp.sum(total, axis=0, keepdims=True) / depth
+        factor = lax.rsqrt(mean + EPSILON)
+
+        @pl.loop(0, depth // STEP)
+        def _(i):
+            at = pl.ds(pl.multiple_of(i * STEP, STEP), STEP)
+            rows = x_ref[at].astype(jnp.float32)
+            normed_ref[at] = (rows * factor * gain_ref[at]).astype(jnp.bfloat16)
+
+    head = head_ref[...]
+    base = step * TILE
+    for start in range(0, tokens, BAND):
+        band = slice(start, start + BAND)
+        logits = jnp.dot(head, normed_ref[:, band], preferred_element_type=jnp.float32)
+        row = base + lax.broadcasted_iota(jnp.int32, logits.shape, 0)
+        wanted = ids_ref[:, band] - offset_ref[0]
+        if vocab % TILE:
+            wanted = jnp.where(wanted < vocab, wanted, -1)
+            logits = jnp.where(row < vocab, logits, NEGATIVE)
+        chosen = jnp.where(row == wanted, logits, 0.0)
+        split = (TILE // 8, 8, BAND)
+        before = max_ref[:, band]
+        best = jnp.maximum(before, jnp.max(logits.reshape(split), axis=0))
+        mass = jnp.sum(jnp.exp(logits.reshape(split) - best[None]), axis=0)
+        max_ref[:, band] = best
+        sum_ref[:, band] = sum_ref[:, band] * jnp.exp(before - best) + mass
+        pick_ref[:, band] += jnp.sum(chosen.reshape(split), axis=0)
+
+
+def logit_stats(x, gain, ids, head, offset):
+    depth, tokens = x.shape
+    vocab = head.shape[0]
+    whole = pl.BlockSpec((8, tokens), lambda v: (0, 0))
     return pl.pallas_call(
         functools.partial(logits_kernel, vocab),
-        out_shape=(jax.ShapeDtypeStruct((rows, 128), jnp.float32),) * 3,
+        out_shape=(jax.ShapeDtypeStruct((8, tokens), jnp.float32),) * 3,
         grid=(pl.cdiv(vocab, TILE),),
         in_specs=[
             pl.BlockSpec(memory_space=pltpu.SMEM),
             pl.BlockSpec(memory_space=VMEM),
             pl.BlockSpec(memory_space=VMEM),
-            pl.BlockSpec((depth, TILE), lambda v: (0, v)),
+            pl.BlockSpec(memory_space=VMEM),
+            pl.BlockSpec((TILE, depth), lambda v: (v, 0)),
         ],
         out_specs=(whole,) * 3,
+        scratch_shapes=[VMEM((depth, tokens), jnp.bfloat16)],
         compiler_params=pltpu.CompilerParams(vmem_limit_bytes=LIMIT),
         name="logits",
-    )(offset, x, ids, head)
+    )(offset, x, gain, ids, head)
 
 
 def stats_kernel(n, x_ref, out_ref, send_sem, recv_sem, local_sem):
@@ -542,16 +572,12 @@
     whole = gather(
         features_kernel, n, planes, hidden_cols, (out_weight.shape[0], total_rows), 2, "features"
     )
-    widened = whole.astype(jnp.float32)
-    factor = lax.rsqrt(jnp.mean(widened * widened, axis=0, keepdims=True) + EPSILON)
-    normed = (widened * factor * norm_gain[:, None]).astype(jnp.bfloat16).T
-
-    ids = by_lane(meta[:, 0, :own_rows]).reshape(total_rows, 1).astype(jnp.int32)
+    ids = by_lane(meta[:, 0, :own_rows]).reshape(1, total_rows).astype(jnp.int32)
     offset = (device_index * lm_head.shape[1]).astype(jnp.int32).reshape(1)
-    peak, mass, pick = logit_stats(normed, ids, lm_head, offset)
-    top = jnp.max(peak, axis=1)
-    mass = jnp.sum(mass * jnp.exp(peak - top[:, None]), axis=1)
-    pick = jnp.sum(pick, axis=1)
+    peak, mass, pick = logit_stats(whole, norm_gain[:, None], ids, lm_head.T, offset)
+    top = jnp.max(peak, axis=0)
+    mass = jnp.sum(mass * jnp.exp(peak - top[None, :]), axis=0)
+    pick = jnp.sum(pick, axis=0)
     stacked = jnp.stack([top, mass, pick]).reshape(3, lanes, planes, own_rows)
     stacked = stacked.transpose(2, 1, 0, 3).reshape(n, 3, own_rows)
     stacked = jnp.pad(stacked, ((0, 0), (0, 5), (0, 128 - own_rows)))

time: 271 us -> 189 us (0.70)
  local copies, waits for them, and re-layouts: 45.6 us -> 7.06 us
  Pallas kernels: 202 us -> 169 us
  other arithmetic: 16.1 us -> 6.41 us
    unnamed x17 -> x12, local copies, waits for them, and re-layouts: 31.7 us -> 0.61 us
    pallas_call x2, Pallas kernels: 104 us -> 80.1 us  [gather(): pl.pallas_call(functools.partial(kernel, n, planes), out_shape=jax.ShapeD...]
    pallas_call x1, Pallas kernels: 17.4 us -> 8.17 us  [stats_exchange(): pl.pallas_call(functools.partial(stats_kernel, n), out_shape=jax.ShapeDty...]
    pallas_call x1 -> x0, local copies, waits for them, and re-layouts: 7.72 us -> none  [gather(): pl.pallas_call(functools.partial(kernel, n, planes), out_shape=jax.ShapeD...]
    reduce_sum x3 -> x2, other arithmetic: 6.53 us -> 1.57 us  [the longest x1 0.8 us: per_device(): mass = jnp.sum(mass * jnp.exp(peak - top[None, :]), axis=0)]
    transpose x1 -> x0, other arithmetic: 3.62 us -> none  [per_device(): normed = (widened * factor * norm_gain[:, None]).astype(jnp.bfloat16).T]
where the time goes in v2:
time: 189 us; the launch traced here: 188 us
  Pallas kernels  169 us (89%)
  local copies, waits for them, and re-layouts  7.06 us (4%)
  other arithmetic  6.41 us (3%)
  matrix products  5.06 us (3%)
    pallas_call x2, Pallas kernels, gather(): pl.pallas_call(functools.partial(kernel, n, planes), out_shape=jax.ShapeD...  80.1 us
    pallas_call x1, Pallas kernels, logit_stats(): pl.pallas_call(functools.partial(logits_kernel, vocab), out_shape=(jax.Sh...  36.8 us
    pallas_call x1, Pallas kernels, exchange(): pl.pallas_call(functools.partial(exchange_kernel, n, planes), out_shape=(...  33.4 us
    pallas_call x1, Pallas kernels, attention(): pl.pallas_call(attention_kernel, out_shape=jax.ShapeDtypeStruct((conts *...  10.2 us
    pallas_call x1, Pallas kernels, stats_exchange(): pl.pallas_call(functools.partial(stats_kernel, n), out_shape=jax.ShapeDty...  8.17 us
    dot_general x1, matrix products, per_device(): lax.dot_general(out_weight, tokens, (((0,), (1,)), ((), ())), preferred_e...  5.06 us

profile of v2, /device:TPU:0, one launch (start us, length us, event | category | flops | bytes accessed | tf_op | source)
XLA Modules:
  0.0 188.0 jit_solution(14469235092072878510)
XLA Ops:
  0.6 0.0 copy-start
  0.7 0.8 reshape_reshape.3
  1.5 0.6 reshape.123.group_ref
  2.1 0.7 convert_element_type.31
  2.8 0.1 convert_element_type.32
  2.9 0.7 scatter.9.meta_ref
  3.6 0.0 copy-start.1
  3.6 0.6 copy-done.1
  4.2 33.4 %exchange.1 = (bf16[8,32,640]{2,1,0:T(8,128)(2,1)}, bf16[8,32,128]{2,1,0:T(8,128)(2,1)}, bf16[8,32,128]{2,1,0:T(8,128)(2,1)}, bf16[2,2048,128]{2,1,0:T(8,128)(2,...) custom-call(bf16[2,32,2560]{2,1,0:T(8,128)(2,1)} %q_ref.1, bf16[2,32,512]{2,1,0:T(8,128)(2,1)} %ck_ref.1, ...), custom_call_target="tpu_custom_call" | custom-call | tf_op jit(solution)/shard_map/exchange/pallas_call | solution.py:262
  37.6 10.2 %attention.1.x_ref = bf16[256,640]{1,0:T(8,128)(2,1)} custom-call(s32[8]{0:T(128)} %reshape.123.group_ref, s32[2]{0:T(128)} %length_ref.1, bf16[8,32,640]{2,1,0:T(8,128)(2,1)} %get-tuple-element.36.q_ref, bf16[8,32,128]{2,1,0:T(8,128)(2,1)} %get-tuple-element.37.ck_ref, bf16[8,32,128]{2,1,0:T(8,128)(2,1)} %get-tuple-element.38.cv_ref, ...), custom_call_target="tpu_custom_call" | custom-call | tf_op jit(solution)/shard_map/attention/pallas_call | solution.py:331
  47.9 41.4 %tokens.1 = bf16[1024,2560]{1,0:T(8,128)(2,1)} custom-call(bf16[256,640]{1,0:T(8,128)(2,1)} %attention.1.x_ref), custom_call_target="tpu_custom_call" | custom-call | tf_op jit(solution)/shard_map/tokens/pallas_call | solution.py:392
  89.2 0.0 copy-done
  89.3 0.0 copy-start.2
  89.3 5.1 %fusion.x_ref = bf16[160,1024]{1,0:T(8,128)(2,1)} fusion(bf16[1024,2560]{1,0:T(8,128)(2,1)} %tokens.1, bf16[2560,160]{0,1:T(8,128)(2,1)S(1)} %copy-done), kind=kOutput, calls=%fused_computation.1 | convolution fusion | flops 839024640 | bytes 6389760 | tf_op jit(solution)/shard_map/dot_general | solution.py:569
  94.3 38.8 %features.1.x_ref = bf16[2560,1024]{1,0:T(8,128)(2,1)} custom-call(bf16[160,1024]{1,0:T(8,128)(2,1)} %fusion.x_ref), custom_call_target="tpu_custom_call" | custom-call | tf_op jit(solution)/shard_map/features/pallas_call | solution.py:392
  133.1 0.8 slice_convert_fusion
  134.0 0.7 convert_element_type.38.ids_ref
  134.6 0.0 copy-done.2
  134.6 1.5 broadcast_in_dim.8.gain_ref
  136.1 0.0 copy-start.3
  136.1 0.0 copy-start.5
  136.1 0.0 copy-start.4
  136.1 36.8 %logits.1 = (f32[8,1024]{1,0:T(8,128)}, f32[8,1024]{1,0:T(8,128)}, f32[8,1024]{1,0:T(8,128)}) custom-call(s32[1]{0:T(128)} %bitcast.offset_ref, bf16[2560,1024]{1,0:T(8,128)(2,1)} %features.1.x_ref, f32[2560,1]{1,0:T(8,128)} %broadcast_in_dim.8.gain_ref, s32[1,1024]{1,0:T(1,128)} %convert_element_type.38.ids_ref, bf16[4752,2560]{1,0:T(8,128)(2,1)} %bitcast.18), custom_call_target="tpu_custom_call" | custom-call | tf_op jit(solution)/shard_map/logits/pallas_call | solution.py:464
  172.9 0.8 reduce_max.18
  173.7 0.8 multiply_reduce_fusion
  174.5 0.1 stack.13
  174.5 0.1 stack.12
  174.6 0.8 reduce_sum.64
  175.4 0.1 stack.14
  175.5 0.6 pad.12.x_ref
  176.1 8.2 %stats.1 = f32[16,8,128]{2,1,0:T(8,128)} custom-call(f32[16,8,128]{2,1,0:T(8,128)} %pad.12.x_ref), custom_call_target="tpu_custom_call" | custom-call | tf_op jit(solution)/shard_map/stats/pallas_call | solution.py:517
  184.3 1.0 slice_reduce_fusion.1
  185.4 0.1 sub.48
  185.5 0.0 copy-done.3
  185.5 0.1 dynamic_slice.5
  185.5 0.9 slice_reduce_fusion
  186.4 0.1 mul.35
  186.5 0.2 fusion.3
  186.7 0.0 copy-done.5
  186.7 0.8 fusion.4
  187.5 0.0 copy-done.4
  187.5 0.5 convert_divide_fusion
  (9 shorter events, 0.1 us)
Async XLA Ops:
  0.6 88.6 %copy-start = (bf16[2560,160]{0,1:T(8,128)(2,1)S(1)}, bf16[2560,160]{0,1:T(8,128)(2,1)}, u32[]{:S(2)}) copy-start(bf16[2560,160]{0,1:T(8,128)(2,1)} %param.22) | copy-start | bytes 2457604
  3.6 0.6 copy-start.1
  89.3 45.4 %copy-start.2 = (f32[2560]{0:T(1024)S(1)}, f32[2560]{0:T(1024)}, u32[]{:S(2)}) copy-start(f32[2560]{0:T(1024)} %param.23) | copy-start | bytes 30724
  136.1 49.3 %copy-start.3 = (s32[32]{0:T(128)S(1)}, s32[32]{0:T(128)}, u32[]{:S(2)}) copy-start(s32[32]{0:T(128)} %param.28) | copy-start | bytes 388
  136.1 50.6 %copy-start.5 = (s32[2]{0:T(128)S(1)}, s32[2]{0:T(128)}, u32[]{:S(2)}) copy-start(s32[2]{0:T(128)} %param.26) | copy-start | bytes 28
  136.1 51.3 %copy-start.4 = (f32[2]{0:T(128)S(1)}, f32[2]{0:T(128)}, u32[]{:S(2)}) copy-start(f32[2]{0:T(128)} %param.29) | copy-start | bytes 28

commit v3 on v2

--- a/solution.py
+++ b/solution.py
@@ -72,7 +72,7 @@
             device_id_type=MESH,
         )
         copy.start()
-        self.sent.append(copy)
+        self.sent.append(part)
 
     def arrived(self, source, part):
         pltpu.make_async_remote_copy(
@@ -110,43 +110,61 @@
             copy.start()
             self.local.append(copy)
 
-    def from_rows(self, plane):
+    def from_rows(self, plane, part):
         at = self.at
-        for part in range(self.parts):
-            for e in range(1, at.half):
-                source = at.device(plane, at.row_at(e), at.core)
-                self.arrived(source, part)
-                self.to_core(self.full(source, part), source, part)
-
-    def from_plane(self, plane, onward):
+        for e in range(1, at.half):
+            source = at.device(plane, at.row_at(e), at.core)
+            self.arrived(source, part)
+            self.to_core(self.full(source, part), source, part)
+
+    def from_plane(self, step, part):
         at = self.at
-        for part in range(self.parts):
-            source = at.device(plane, at.row, at.core)
-            self.arrived(source, part)
-            if onward:
-                target = at.device(at.plane_at(1), at.row, at.core)
-                self.send(self.full(source, part), source, part, target)
-            self.to_rows(self.full(source, part), source, part)
-            self.to_core(self.full(source, part), source, part)
-
-    def finish(self):
+        source = at.device(at.plane_at(step), at.row, at.core)
+        self.arrived(source, part)
+        if self.ring and step > 1:
+            target = at.device(at.plane_at(1), at.row, at.core)
+            self.send(self.full(source, part), source, part, target)
+        self.to_rows(self.full(source, part), source, part)
+        self.to_core(self.full(source, part), source, part)
+
+    def events(self, part):
         at = self.at
         steps = [1, at.planes - 1] + list(range(2, at.planes - 1))
         if self.ring:
             steps = list(range(at.planes - 1, 0, -1))
-        order = [at.plane_at(d) for d in steps]
-        self.from_rows(at.plane)
-        for i, plane in enumerate(order):
-            self.from_plane(plane, self.ring and steps[i] > 1)
+        listed = [functools.partial(self.from_rows, at.plane, part)]
+        for i, step in enumerate(steps):
+            listed.append(functools.partial(self.from_plane, step, part))
             if i >= 1:
-                self.from_rows(order[i - 1])
-        self.from_rows(order[-1])
+                listed.append(functools.partial(self.from_rows, at.plane_at(steps[i - 1]), part))
+        listed.append(functools.partial(self.from_rows, at.plane_at(steps[-1]), part))
+        return listed
+
+    def from_core(self, part):
+        at = self.at
         for plane in range(at.planes):
             for row in range(at.half):
-                for part in range(self.parts):
-                    self.arrived(at.device(plane, row, 1 - at.core), part)
-        for copy in self.sent:
-            copy.wait_send()
+                self.arrived(at.device(plane, row, 1 - at.core), part)
+
+    def drain(self):
+        at = self.at
+        for i, part in enumerate(self.sent):
+            pltpu.make_async_remote_copy(
+                src_ref=self.full(at.me, part),
+                dst_ref=self.full(at.me, part),
+                send_sem=self.send_sem.at[i],
+                recv_sem=self.recv_sem.at[0],
+                device_id={"seq": at.device(at.plane, at.row, 1 - at.core)},
+                device_id_type=MESH,
+            ).wait_send()
+
+    def finish(self):
+        for both in zip(*[self.events(part) for part in range(self.parts)]):
+            for event in both:
+                event()
+        for part in range(self.parts):
+            self.from_core(part)
+        self.drain()
         for copy in self.local:
             copy.wait()
 
@@ -369,24 +387,6 @@
     spread.finish()
 
 
-def features_kernel(n, planes, x_ref, out_ref, send_sem, recv_sem, local_sem):
-    at = Place(n, planes)
-    greet(at.peers())
-    rows, width = x_ref.shape
-    piece = width // PARTS
-
-    def own(part, plane):
-        return x_ref.at[:, pl.ds(part * piece, piece)]
-
-    def full(source, part):
-        start = pl.multiple_of(source * rows, 16)
-        return out_ref.at[pl.ds(start, rows), pl.ds(part * piece, piece)]
-
-    spread = Spread(at, PARTS, own, full, send_sem, recv_sem, local_sem)
-    spread.start()
-    spread.finish()
-
-
 def gather(kernel, n, planes, x, shape, number, name):
     dma = pltpu.SemaphoreType.DMA
     return pl.pallas_call(
@@ -407,86 +407,182 @@
 
 
 TILE = 528
-BAND = 512
+BAND = 256
 STEP = 128
 
 
-def logits_kernel(
-    vocab, offset_ref, x_ref, gain_ref, ids_ref, head_ref, max_ref, sum_ref, pick_ref, normed_ref
+def scores_kernel(
+    n,
+    planes,
+    offset_ref,
+    x_ref,
+    gain_ref,
+    ids_ref,
+    head_hbm,
+    out_ref,
+    hidden_ref,
+    normed_ref,
+    head_ref,
+    max_ref,
+    sum_ref,
+    pick_ref,
+    send_sem,
+    recv_sem,
+    local_sem,
+    head_sem,
 ):
-    step = pl.program_id(0)
-    depth, tokens = x_ref.shape
-
-    @pl.when(step == 0)
-    def _():
-        max_ref[...] = jnp.full_like(max_ref, NEGATIVE)
-        sum_ref[...] = jnp.zeros_like(sum_ref)
-        pick_ref[...] = jnp.zeros_like(pick_ref)
+    at = Place(n, planes)
+    greet(at.peers())
+    rows, tokens = x_ref.shape
+    depth = rows * n
+    vocab = head_hbm.shape[0]
+    piece = tokens // PARTS
+    tiles, rest = vocab // TILE, vocab % TILE
+
+    def own(part, plane):
+        return x_ref.at[:, pl.ds(part * piece, piece)]
+
+    def full(source, part):
+        start = pl.multiple_of(source * rows, 16)
+        return hidden_ref.at[pl.ds(start, rows), pl.ds(part * piece, piece)]
+
+    spread = Spread(at, PARTS, own, full, send_sem, recv_sem, local_sem)
+    spread.start()
+
+    def load(tile, size):
+        cut = pl.ds(pl.multiple_of(tile * TILE, 8), size)
+        return pltpu.make_async_copy(head_hbm.at[cut], head_ref.at[cut], head_sem.at[tile])
+
+    for tile in range(tiles):
+        load(tile, TILE).start()
+    if rest:
+        load(tiles, rest).start()
+
+    max_ref[...] = jnp.full_like(max_ref, NEGATIVE)
+    sum_ref[...] = jnp.zeros_like(sum_ref)
+    pick_ref[...] = jnp.zeros_like(pick_ref)
+
+    def normalize(part):
+        columns = pl.ds(part * piece, piece)
 
         def square(i, total):
-            rows = x_ref[pl.ds(pl.multiple_of(i * STEP, STEP), STEP)].astype(jnp.float32)
-            return total + jnp.sum((rows * rows).reshape(STEP // 8, 8, tokens), axis=0)
-
-        total = lax.fori_loop(0, depth // STEP, square, jnp.zeros((8, tokens), jnp.float32))
-        mean = jnp.sum(total, axis=0, keepdims=True) / depth
-        factor = lax.rsqrt(mean + EPSILON)
+            cut = pl.ds(pl.multiple_of(i * STEP, STEP), STEP)
+            wide = hidden_ref[cut, columns].astype(jnp.float32)
+            return total + jnp.sum((wide * wide).reshape(STEP // 8, 8, piece), axis=0)
+
+        total = lax.fori_loop(0, depth // STEP, square, jnp.zeros((8, piece), jnp.float32))
+        factor = lax.rsqrt(jnp.sum(total, axis=0, keepdims=True) / depth + EPSILON)
 
         @pl.loop(0, depth // STEP)
         def _(i):
-            at = pl.ds(pl.multiple_of(i * STEP, STEP), STEP)
-            rows = x_ref[at].astype(jnp.float32)
-            normed_ref[at] = (rows * factor * gain_ref[at]).astype(jnp.bfloat16)
-
-    head = head_ref[...]
-    base = step * TILE
-    for start in range(0, tokens, BAND):
-        band = slice(start, start + BAND)
-        logits = jnp.dot(head, normed_ref[:, band], preferred_element_type=jnp.float32)
-        row = base + lax.broadcasted_iota(jnp.int32, logits.shape, 0)
-        wanted = ids_ref[:, band] - offset_ref[0]
-        if vocab % TILE:
-            wanted = jnp.where(wanted < vocab, wanted, -1)
-            logits = jnp.where(row < vocab, logits, NEGATIVE)
-        chosen = jnp.where(row == wanted, logits, 0.0)
-        split = (TILE // 8, 8, BAND)
-        before = max_ref[:, band]
-        best = jnp.maximum(before, jnp.max(logits.reshape(split), axis=0))
-        mass = jnp.sum(jnp.exp(logits.reshape(split) - best[None]), axis=0)
-        max_ref[:, band] = best
-        sum_ref[:, band] = sum_ref[:, band] * jnp.exp(before - best) + mass
-        pick_ref[:, band] += jnp.sum(chosen.reshape(split), axis=0)
-
-
-def logit_stats(x, gain, ids, head, offset):
-    depth, tokens = x.shape
-    vocab = head.shape[0]
-    whole = pl.BlockSpec((8, tokens), lambda v: (0, 0))
+            cut = pl.ds(pl.multiple_of(i * STEP, STEP), STEP)
+            wide = hidden_ref[cut, columns].astype(jnp.float32)
+            normed_ref[cut] = (wide * factor * gain_ref[cut]).astype(jnp.bfloat16)
+
+    def score(part, tile, size):
+        if part == 0:
+            load(tile, size).wait()
+        head = head_ref[pl.ds(pl.multiple_of(tile * TILE, 8), size)]
+        base = tile * TILE + offset_ref[0]
+        products = [
+            jnp.dot(head, normed_ref[:, start : start + BAND], preferred_element_type=jnp.float32)
+            for start in range(0, piece, BAND)
+        ]
+        for i, logits in enumerate(products):
+            band = slice(part * piece + i * BAND, part * piece + (i + 1) * BAND)
+            row = lax.broadcasted_iota(jnp.int32, logits.shape, 0)
+            chosen = jnp.where(row == ids_ref[:, band] - base, logits, 0.0)
+            split = (size // 8, 8, BAND)
+            before = max_ref[:, band]
+            best = jnp.maximum(before, jnp.max(logits.reshape(split), axis=0))
+            mass = jnp.sum(jnp.exp(logits.reshape(split) - best[None]), axis=0)
+            max_ref[:, band] = best
+            sum_ref[:, band] = sum_ref[:, band] * jnp.exp(before - best) + mass
+            pick_ref[:, band] += jnp.sum(chosen.reshape(split), axis=0)
+
+    def score_all(part, events):
+        @pl.loop(0, tiles)
+        def _(tile):
+            for i, event in enumerate(events):
+                pl.when(tile == min(i, tiles - 1))(event)
+            score(part, tile, TILE)
+
+        if rest:
+            score(part, tiles, rest)
+
+    first, second = spread.events(0), spread.events(1)
+    cut = len(first) - 2
+    for event in first[:cut] + second[:2] + first[cut:]:
+        event()
+    spread.from_core(0)
+    second[2]()
+    spread.local[0].wait()
+    normalize(0)
+    score_all(0, second[3:])
+    spread.from_core(1)
+    spread.local[1].wait()
+    normalize(1)
+    score_all(1, [])
+    spread.drain()
+    peak = max_ref[...]
+    top = jnp.max(peak, axis=0, keepdims=True)
+    out_ref[...] = jnp.zeros_like(out_ref)
+    out_ref[0:1] = top
+    out_ref[1:2] = jnp.sum(sum_ref[...] * jnp.exp(peak - top), axis=0, keepdims=True)
+    out_ref[2:3] = jnp.sum(pick_ref[...], axis=0, keepdims=True)
+
+
+def scores(n, planes, x, gain, ids, head, offset):
+    rows, tokens = x.shape
+    depth = rows * n
+    dma = pltpu.SemaphoreType.DMA
+    vmem = pl.BlockSpec(memory_space=VMEM)
+    running = VMEM((8, tokens), jnp.float32)
     return pl.pallas_call(
-        functools.partial(logits_kernel, vocab),
-        out_shape=(jax.ShapeDtypeStruct((8, tokens), jnp.float32),) * 3,
-        grid=(pl.cdiv(vocab, TILE),),
+        functools.partial(scores_kernel, n, planes),
+        out_shape=jax.ShapeDtypeStruct((8, tokens), jnp.float32),
         in_specs=[
             pl.BlockSpec(memory_space=pltpu.SMEM),
-            pl.BlockSpec(memory_space=VMEM),
-            pl.BlockSpec(memory_space=VMEM),
-            pl.BlockSpec(memory_space=VMEM),
-            pl.BlockSpec((TILE, depth), lambda v: (v, 0)),
+            vmem,
+            vmem,
+            vmem,
+            pl.BlockSpec(memory_space=pl.ANY),
         ],
-        out_specs=(whole,) * 3,
-        scratch_shapes=[VMEM((depth, tokens), jnp.bfloat16)],
-        compiler_params=pltpu.CompilerParams(vmem_limit_bytes=LIMIT),
-        name="logits",
+        out_specs=vmem,
+        scratch_shapes=[
+            VMEM((depth, tokens), x.dtype),
+            VMEM((depth, tokens // PARTS), x.dtype),
+            VMEM(head.shape, head.dtype),
+            running,
+            running,
+            running,
+            dma((PARTS * send_count(n, planes),)),
+            dma((PARTS * n,)),
+            dma((PARTS,)),
+            dma((pl.cdiv(head.shape[0], TILE),)),
+        ],
+        compiler_params=pltpu.CompilerParams(
+            collective_id=2, has_side_effects=True, vmem_limit_bytes=LIMIT
+        ),
+        name="scores",
     )(offset, x, gain, ids, head)
 
 
-def stats_kernel(n, x_ref, out_ref, send_sem, recv_sem, local_sem):
+def stats_kernel(n, planes, x_ref, out_ref, send_sem, recv_sem, local_sem):
     me = lax.axis_index("seq")
     greet([(me + d) % n for d in range(1, n)])
+    lanes = n // planes
+    share = x_ref.shape[1] // n
+
+    def block(owner):
+        place = (owner % lanes) * planes + owner // lanes
+        return x_ref.at[:, pl.ds(pl.multiple_of(place * share // 128 * 128, 128), 128)]
+
     sent = []
     for d in range(1, n):
         target = (me + d) % n
         copy = pltpu.make_async_remote_copy(
-            src_ref=x_ref.at[target],
+            src_ref=block(target),
             dst_ref=out_ref.at[me],
             send_sem=send_sem.at[d],
             recv_sem=recv_sem.at[me],
@@ -495,12 +591,12 @@
         )
         copy.start()
         sent.append(copy)
-    local = pltpu.make_async_copy(x_ref.at[me], out_ref.at[me], local_sem)
+    local = pltpu.make_async_copy(block(me), out_ref.at[me], local_sem)
     local.start()
     for d in range(1, n):
         source = (me + d) % n
         pltpu.make_async_remote_copy(
-            src_ref=x_ref.at[source],
+            src_ref=out_ref.at[source],
             dst_ref=out_ref.at[source],
             send_sem=send_sem.at[d],
             recv_sem=recv_sem.at[source],
@@ -512,11 +608,11 @@
     local.wait()
 
 
-def stats_exchange(n, x):
+def stats_exchange(n, planes, x):
     dma = pltpu.SemaphoreType.DMA
     return pl.pallas_call(
-        functools.partial(stats_kernel, n),
-        out_shape=jax.ShapeDtypeStruct(x.shape, x.dtype),
+        functools.partial(stats_kernel, n, planes),
+        out_shape=jax.ShapeDtypeStruct((n, x.shape[0], 128), x.dtype),
         in_specs=[pl.BlockSpec(memory_space=VMEM)],
         out_specs=pl.BlockSpec(memory_space=VMEM),
         scratch_shapes=[dma((n,)), dma((n,)), dma],
@@ -569,19 +665,13 @@
     hidden_cols = lax.dot_general(
         out_weight, tokens, (((0,), (1,)), ((), ())), preferred_element_type=jnp.float32
     ).astype(jnp.bfloat16)
-    whole = gather(
-        features_kernel, n, planes, hidden_cols, (out_weight.shape[0], total_rows), 2, "features"
-    )
     ids = by_lane(meta[:, 0, :own_rows]).reshape(1, total_rows).astype(jnp.int32)
     offset = (device_index * lm_head.shape[1]).astype(jnp.int32).reshape(1)
-    peak, mass, pick = logit_stats(whole, norm_gain[:, None], ids, lm_head.T, offset)
-    top = jnp.max(peak, axis=0)
-    mass = jnp.sum(mass * jnp.exp(peak - top[None, :]), axis=0)
-    pick = jnp.sum(pick, axis=0)
-    stacked = jnp.stack([top, mass, pick]).reshape(3, lanes, planes, own_rows)
-    stacked = stacked.transpose(2, 1, 0, 3).reshape(n, 3, own_rows)
-    stacked = jnp.pad(stacked, ((0, 0), (0, 5), (0, 128 - own_rows)))
-    shares = stats_exchange(n, stacked)[:, :3, :own_rows]
+    stats = scores(n, planes, hidden_cols, norm_gain[:, None], ids, lm_head.T, offset)
+    place = lane * planes + device_index // lanes
+    shares = lax.dynamic_slice_in_dim(
+        stats_exchange(n, planes, stats), place * own_rows % 128, own_rows, axis=2
+    )
     maximum = jnp.max(shares[:, 0], axis=0)
     total_mass = jnp.sum(shares[:, 1] * jnp.exp(shares[:, 0] - maximum[None, :]), axis=0)
     picked = jnp.sum(shares[:, 2], axis=0)

time: 189 us -> 179 us (0.947)
  Pallas kernels: 169 us -> 162 us
  other arithmetic: 6.41 us -> 4.16 us
    pallas_call x2 -> x1, Pallas kernels: 80.1 us -> 41.4 us  [gather(): pl.pallas_call(functools.partial(kernel, n, planes), out_shape=jax.ShapeD...]
    pallas_call x2, Pallas kernels: 44.9 us -> 77.5 us  [the longest x1 69.4 us: scores(): pl.pallas_call(functools.partial(scores_kernel, n, planes), out_shape=jax...]
where the time goes in v3:
time: 179 us
  Pallas kernels  162 us (91%)
  local copies, waits for them, and re-layouts  6.14 us (3%)
  matrix products  5.06 us (3%)
  other arithmetic  4.16 us (2%)
    pallas_call x1, Pallas kernels, scores(): pl.pallas_call(functools.partial(scores_kernel, n, planes), out_shape=jax...  69.4 us
    pallas_call x1, Pallas kernels, gather(): pl.pallas_call(functools.partial(kernel, n, planes), out_shape=jax.ShapeD...  41.4 us
    pallas_call x1, Pallas kernels, exchange(): pl.pallas_call(functools.partial(exchange_kernel, n, planes), out_shape=(...  33.4 us
    pallas_call x1, Pallas kernels, attention(): pl.pallas_call(attention_kernel, out_shape=jax.ShapeDtypeStruct((conts *...  10.2 us
    pallas_call x1, Pallas kernels, stats_exchange(): pl.pallas_call(functools.partial(stats_kernel, n, planes), out_shape=jax....  8.08 us
    dot_general x1, matrix products, per_device(): lax.dot_general(out_weight, tokens, (((0,), (1,)), ((), ())), preferred_e...  5.06 us

profile of v3, /device:TPU:0, one launch (start us, length us, event | category | flops | bytes accessed | tf_op | source)
XLA Modules:
  0.0 178.6 jit_solution(8868666981619677489)
XLA Ops:
  0.6 0.0 copy-start
  0.7 0.8 reshape_reshape.3
  1.5 0.6 reshape.112.group_ref
  2.1 0.7 convert_element_type.29
  2.8 0.1 convert_element_type.30
  2.9 0.7 scatter.9.meta_ref
  3.6 0.0 copy-start.1
  3.6 0.6 copy-done.1
  4.2 33.4 %exchange.1 = (bf16[8,32,640]{2,1,0:T(8,128)(2,1)}, bf16[8,32,128]{2,1,0:T(8,128)(2,1)}, bf16[8,32,128]{2,1,0:T(8,128)(2,1)}, bf16[2,2048,128]{2,1,0:T(8,128)(2,...) custom-call(bf16[2,32,2560]{2,1,0:T(8,128)(2,1)} %q_ref.1, bf16[2,32,512]{2,1,0:T(8,128)(2,1)} %ck_ref.1, ...), custom_call_target="tpu_custom_call" | custom-call | tf_op jit(solution)/shard_map/exchange/pallas_call | solution.py:280
  37.6 10.2 %attention.1.x_ref = bf16[256,640]{1,0:T(8,128)(2,1)} custom-call(s32[8]{0:T(128)} %reshape.112.group_ref, s32[2]{0:T(128)} %length_ref.1, bf16[8,32,640]{2,1,0:T(8,128)(2,1)} %get-tuple-element.33.q_ref, bf16[8,32,128]{2,1,0:T(8,128)(2,1)} %get-tuple-element.34.ck_ref, bf16[8,32,128]{2,1,0:T(8,128)(2,1)} %get-tuple-element.35.cv_ref, ...), custom_call_target="tpu_custom_call" | custom-call | tf_op jit(solution)/shard_map/attention/pallas_call | solution.py:349
  47.9 0.0 copy-start.2
  47.9 41.4 %tokens.1 = bf16[1024,2560]{1,0:T(8,128)(2,1)} custom-call(bf16[256,640]{1,0:T(8,128)(2,1)} %attention.1.x_ref), custom_call_target="tpu_custom_call" | custom-call | tf_op jit(solution)/shard_map/tokens/pallas_call | solution.py:392
  89.3 0.0 copy-done
  89.3 5.1 %fusion.x_ref = bf16[160,1024]{1,0:T(8,128)(2,1)} fusion(bf16[1024,2560]{1,0:T(8,128)(2,1)} %tokens.1, bf16[2560,160]{0,1:T(8,128)(2,1)S(1)} %copy-done), kind=kOutput, calls=%fused_computation.1 | convolution fusion | flops 839024640 | bytes 6389760 | tf_op jit(solution)/shard_map/dot_general | solution.py:665
  94.3 0.8 slice_convert_fusion
  95.2 0.7 convert_element_type.36.ids_ref
  95.8 0.0 copy-done.2
  95.9 1.5 broadcast_in_dim.8.gain_ref
  97.3 0.0 copy-start.3
  97.3 0.0 copy-start.5
  97.3 0.0 copy-start.4
  97.3 69.4 %scores.1.x_ref = f32[8,1024]{1,0:T(8,128)} custom-call(s32[1]{0:T(128)} %bitcast.offset_ref, bf16[160,1024]{1,0:T(8,128)(2,1)} %fusion.x_ref, f32[2560,1]{1,0:T(8,128)} %broadcast_in_dim.8.gain_ref, s32[1,1024]{1,0:T(1,128)} %convert_element_type.36.ids_ref, bf16[4752,2560]{1,0:T(8,128)(2,1)} %bitcast.15), custom_call_target="tpu_custom_call" | custom-call | tf_op jit(solution)/shard_map/scores/pallas_call | solution.py:541
  166.7 8.1 %stats.1 = f32[16,8,128]{2,1,0:T(8,128)} custom-call(f32[8,1024]{1,0:T(8,128)} %scores.1.x_ref), custom_call_target="tpu_custom_call" | custom-call | tf_op jit(solution)/shard_map/stats/pallas_call | solution.py:613
  174.8 1.1 dynamic-slice_reduce_fusion
  176.0 0.1 sub.43
  176.1 0.0 copy-done.3
  176.1 0.1 dynamic_slice.9
  176.1 0.9 slice_reduce_fusion
  177.0 0.1 mul.39
  177.1 0.2 fusion.3
  177.3 0.0 copy-done.5
  177.3 0.8 fusion.4
  178.1 0.0 copy-done.4
  178.1 0.5 convert_divide_fusion
  (7 shorter events, 0.1 us)
Async XLA Ops:
  0.6 88.6 %copy-start = (bf16[2560,160]{0,1:T(8,128)(2,1)S(1)}, bf16[2560,160]{0,1:T(8,128)(2,1)}, u32[]{:S(2)}) copy-start(bf16[2560,160]{0,1:T(8,128)(2,1)} %param.22) | copy-start | bytes 2457604
  3.6 0.6 copy-start.1
  47.9 48.0 %copy-start.2 = (f32[2560]{0:T(1024)S(1)}, f32[2560]{0:T(1024)}, u32[]{:S(2)}) copy-start(f32[2560]{0:T(1024)} %param.23) | copy-start | bytes 30724
  97.3 78.7 %copy-start.3 = (s32[32]{0:T(128)S(1)}, s32[32]{0:T(128)}, u32[]{:S(2)}) copy-start(s32[32]{0:T(128)} %param.28) | copy-start | bytes 388
  97.3 80.0 %copy-start.5 = (s32[2]{0:T(128)S(1)}, s32[2]{0:T(128)}, u32[]{:S(2)}) copy-start(s32[2]{0:T(128)} %param.26) | copy-start | bytes 28
  97.3 80.8 %copy-start.4 = (f32[2]{0:T(128)S(1)}, f32[2]{0:T(128)}, u32[]{:S(2)}) copy-start(f32[2]{0:T(128)} %param.29) | copy-start | bytes 28

commit v4 on v3

--- a/solution.py
+++ b/solution.py
@@ -94,21 +94,23 @@
         self.send(src_ref, source, part, at.device(at.plane, at.row, 1 - at.core))
 
     def start(self):
-        at = self.at
-        self.local = []
         for part in range(self.parts):
-            for d in range(1, 2 if self.ring else at.planes):
-                target = at.plane_at(d)
-                self.send(
-                    self.own(part, target), at.me, part, at.device(target, at.row, at.core)
-                )
-            self.to_rows(self.own(part, at.plane), at.me, part)
-            self.to_core(self.own(part, at.plane), at.me, part)
-            copy = pltpu.make_async_copy(
-                self.own(part, at.plane), self.full(at.me, part), self.local_sem.at[part]
-            )
-            copy.start()
-            self.local.append(copy)
+            self.start_part(part)
+
+    def start_part(self, part):
+        at = self.at
+        for d in range(1, 2 if self.ring else at.planes):
+            target = at.plane_at(d)
+            self.send(self.own(part, target), at.me, part, at.device(target, at.row, at.core))
+        self.to_rows(self.own(part, at.plane), at.me, part)
+        self.to_core(self.own(part, at.plane), at.me, part)
+        self.keep(part).start()
+
+    def keep(self, part):
+        at = self.at
+        return pltpu.make_async_copy(
+            self.own(part, at.plane), self.full(at.me, part), self.local_sem.at[part]
+        )
 
     def from_rows(self, plane, part):
         at = self.at
@@ -165,8 +167,8 @@
         for part in range(self.parts):
             self.from_core(part)
         self.drain()
-        for copy in self.local:
-            copy.wait()
+        for part in range(self.parts):
+            self.keep(part).wait()
 
 
 def exchange_kernel(
@@ -406,7 +408,9 @@
     )(x)
 
 
-TILE = 528
+TILE = 1584
+SUB = 528
+CUTS = 4
 BAND = 256
 STEP = 128
 
@@ -436,7 +440,7 @@
     rows, tokens = x_ref.shape
     depth = rows * n
     vocab = head_hbm.shape[0]
-    piece = tokens // PARTS
+    piece = tokens // CUTS
     tiles, rest = vocab // TILE, vocab % TILE
 
     def own(part, plane):
@@ -446,8 +450,9 @@
         start = pl.multiple_of(source * rows, 16)
         return hidden_ref.at[pl.ds(start, rows), pl.ds(part * piece, piece)]
 
-    spread = Spread(at, PARTS, own, full, send_sem, recv_sem, local_sem)
-    spread.start()
+    spread = Spread(at, CUTS, own, full, send_sem, recv_sem, local_sem)
+    spread.start_part(0)
+    spread.start_part(1)
 
     def load(tile, size):
         cut = pl.ds(pl.multiple_of(tile * TILE, 8), size)
@@ -482,47 +487,66 @@
     def score(part, tile, size):
         if part == 0:
             load(tile, size).wait()
-        head = head_ref[pl.ds(pl.multiple_of(tile * TILE, 8), size)]
         base = tile * TILE + offset_ref[0]
-        products = [
-            jnp.dot(head, normed_ref[:, start : start + BAND], preferred_element_type=jnp.float32)
-            for start in range(0, piece, BAND)
-        ]
-        for i, logits in enumerate(products):
-            band = slice(part * piece + i * BAND, part * piece + (i + 1) * BAND)
-            row = lax.broadcasted_iota(jnp.int32, logits.shape, 0)
-            chosen = jnp.where(row == ids_ref[:, band] - base, logits, 0.0)
-            split = (size // 8, 8, BAND)
-            before = max_ref[:, band]
+
+        def product(start, width, band):
+            at_row = pl.ds(pl.multiple_of(tile * TILE + start, 8), width)
+            return jnp.dot(
+                head_ref[at_row], normed_ref[:, band], preferred_element_type=jnp.float32
+            )
+
+        def absorb(start, width, band, logits):
+            columns = slice(part * piece + band.start, part * piece + band.stop)
+            row = start + lax.broadcasted_iota(jnp.int32, logits.shape, 0)
+            chosen = jnp.where(row == ids_ref[:, columns] - base, logits, 0.0)
+            split = (width // 8, 8, BAND)
+            before = max_ref[:, columns]
             best = jnp.maximum(before, jnp.max(logits.reshape(split), axis=0))
             mass = jnp.sum(jnp.exp(logits.reshape(split) - best[None]), axis=0)
-            max_ref[:, band] = best
-            sum_ref[:, band] = sum_ref[:, band] * jnp.exp(before - best) + mass
-            pick_ref[:, band] += jnp.sum(chosen.reshape(split), axis=0)
+            max_ref[:, columns] = best
+            sum_ref[:, columns] = sum_ref[:, columns] * jnp.exp(before - best) + mass
+            pick_ref[:, columns] += jnp.sum(chosen.reshape(split), axis=0)
+
+        pending = None
+        for begin in range(0, piece, BAND):
+            for start in range(0, size, SUB):
+                job = (start, min(SUB, size - start), slice(begin, begin + BAND))
+                logits = product(*job)
+                if pending is not None:
+                    absorb(*pending)
+                pending = job + (logits,)
+        absorb(*pending)
 
     def score_all(part, events):
+        each = -(-len(events) // max(tiles, 1))
+
         @pl.loop(0, tiles)
         def _(tile):
             for i, event in enumerate(events):
-                pl.when(tile == min(i, tiles - 1))(event)
+                pl.when(tile == i // each)(event)
             score(part, tile, TILE)
 
         if rest:
             score(part, tiles, rest)
 
-    first, second = spread.events(0), spread.events(1)
-    cut = len(first) - 2
-    for event in first[:cut] + second[:2] + first[cut:]:
+    listed = [spread.events(part) for part in range(CUTS)]
+    rows0, za0, zb0, ya0, zc0 = listed[0][:5]
+    early = [rows0, za0, zb0] + listed[1][:2] + [ya0, zc0] + listed[1][2:3]
+    early += [functools.partial(spread.start_part, 2)] + listed[0][5:]
+    for event in early:
         event()
-    spread.from_core(0)
-    second[2]()
-    spread.local[0].wait()
-    normalize(0)
-    score_all(0, second[3:])
-    spread.from_core(1)
-    spread.local[1].wait()
-    normalize(1)
-    score_all(1, [])
+    for part in range(CUTS):
+        spread.from_core(part)
+        spread.keep(part).wait()
+        normalize(part)
+        beside = []
+        if part + 1 < CUTS:
+            now = listed[part + 1][3:]
+            after = listed[part + 2][:3] if part + 2 < CUTS else [None] * 3
+            beside = [now[0], now[1], after[0], after[1], now[2], after[2]] + now[3:]
+            if part + 3 < CUTS:
+                beside.append(functools.partial(spread.start_part, part + 3))
+        score_all(part, [event for event in beside if event is not None])
     spread.drain()
     peak = max_ref[...]
     top = jnp.max(peak, axis=0, keepdims=True)
@@ -551,14 +575,14 @@
         out_specs=vmem,
         scratch_shapes=[
             VMEM((depth, tokens), x.dtype),
-            VMEM((depth, tokens // PARTS), x.dtype),
+            VMEM((depth, tokens // CUTS), x.dtype),
             VMEM(head.shape, head.dtype),
             running,
             running,
             running,
-            dma((PARTS * send_count(n, planes),)),
-            dma((PARTS * n,)),
-            dma((PARTS,)),
+            dma((CUTS * send_count(n, planes),)),
+            dma((CUTS * n,)),
+            dma((CUTS,)),
             dma((pl.cdiv(head.shape[0], TILE),)),
         ],
         compiler_params=pltpu.CompilerParams(

time: 179 us -> 179 us (level)
  no operation moved by 1% of the time
where the time goes in v4:
time: 179 us
  Pallas kernels  163 us (91%)
  local copies, waits for them, and re-layouts  6.14 us (3%)
  matrix products  5.06 us (3%)
  other arithmetic  4.16 us (2%)
    pallas_call x1, Pallas kernels, scores(): pl.pallas_call(functools.partial(scores_kernel, n, planes), out_shape=jax...  69.5 us
    pallas_call x1, Pallas kernels, gather(): pl.pallas_call(functools.partial(kernel, n, planes), out_shape=jax.ShapeD...  41.4 us
    pallas_call x1, Pallas kernels, exchange(): pl.pallas_call(functools.partial(exchange_kernel, n, planes), out_shape=(...  33.4 us
    pallas_call x1, Pallas kernels, attention(): pl.pallas_call(attention_kernel, out_shape=jax.ShapeDtypeStruct((conts *...  10.2 us
    pallas_call x1, Pallas kernels, stats_exchange(): pl.pallas_call(functools.partial(stats_kernel, n, planes), out_shape=jax....  8.03 us
    dot_general x1, matrix products, per_device(): lax.dot_general(out_weight, tokens, (((0,), (1,)), ((), ())), preferred_e...  5.06 us

profile of v4, /device:TPU:0, one launch (start us, length us, event | category | flops | bytes accessed | tf_op | source)
XLA Modules:
  0.0 178.7 jit_solution(13691125771367452912)
XLA Ops:
  0.6 0.0 copy-start
  0.7 0.8 reshape_reshape.3
  1.5 0.6 reshape.112.group_ref
  2.1 0.7 convert_element_type.29
  2.8 0.1 convert_element_type.30
  2.9 0.7 scatter.9.meta_ref
  3.6 0.0 copy-start.1
  3.6 0.6 copy-done.1
  4.2 33.4 %exchange.1 = (bf16[8,32,640]{2,1,0:T(8,128)(2,1)}, bf16[8,32,128]{2,1,0:T(8,128)(2,1)}, bf16[8,32,128]{2,1,0:T(8,128)(2,1)}, bf16[2,2048,128]{2,1,0:T(8,128)(2,...) custom-call(bf16[2,32,2560]{2,1,0:T(8,128)(2,1)} %q_ref.1, bf16[2,32,512]{2,1,0:T(8,128)(2,1)} %ck_ref.1, ...), custom_call_target="tpu_custom_call" | custom-call | tf_op jit(solution)/shard_map/exchange/pallas_call | solution.py:282
  37.6 10.2 %attention.1.x_ref = bf16[256,640]{1,0:T(8,128)(2,1)} custom-call(s32[8]{0:T(128)} %reshape.112.group_ref, s32[2]{0:T(128)} %length_ref.1, bf16[8,32,640]{2,1,0:T(8,128)(2,1)} %get-tuple-element.33.q_ref, bf16[8,32,128]{2,1,0:T(8,128)(2,1)} %get-tuple-element.34.ck_ref, bf16[8,32,128]{2,1,0:T(8,128)(2,1)} %get-tuple-element.35.cv_ref, ...), custom_call_target="tpu_custom_call" | custom-call | tf_op jit(solution)/shard_map/attention/pallas_call | solution.py:351
  47.9 0.0 copy-start.2
  47.9 41.4 %tokens.1 = bf16[1024,2560]{1,0:T(8,128)(2,1)} custom-call(bf16[256,640]{1,0:T(8,128)(2,1)} %attention.1.x_ref), custom_call_target="tpu_custom_call" | custom-call | tf_op jit(solution)/shard_map/tokens/pallas_call | solution.py:394
  89.3 0.0 copy-done
  89.3 5.1 %fusion.x_ref = bf16[160,1024]{1,0:T(8,128)(2,1)} fusion(bf16[1024,2560]{1,0:T(8,128)(2,1)} %tokens.1, bf16[2560,160]{0,1:T(8,128)(2,1)S(1)} %copy-done), kind=kOutput, calls=%fused_computation.1 | convolution fusion | flops 839024640 | bytes 6389760 | tf_op jit(solution)/shard_map/dot_general | solution.py:689
  94.3 0.8 slice_convert_fusion
  95.2 0.7 convert_element_type.36.ids_ref
  95.8 0.0 copy-done.2
  95.9 1.5 broadcast_in_dim.8.gain_ref
  97.3 0.0 copy-start.3
  97.3 0.0 copy-start.5
  97.3 0.0 copy-start.4
  97.3 69.5 %scores.1.x_ref = f32[8,1024]{1,0:T(8,128)} custom-call(s32[1]{0:T(128)} %bitcast.offset_ref, bf16[160,1024]{1,0:T(8,128)(2,1)} %fusion.x_ref, f32[2560,1]{1,0:T(8,128)} %broadcast_in_dim.8.gain_ref, s32[1,1024]{1,0:T(1,128)} %convert_element_type.36.ids_ref, bf16[4752,2560]{1,0:T(8,128)(2,1)} %bitcast.15), custom_call_target="tpu_custom_call" | custom-call | tf_op jit(solution)/shard_map/scores/pallas_call | solution.py:565
  166.9 8.0 %stats.1 = f32[16,8,128]{2,1,0:T(8,128)} custom-call(f32[8,1024]{1,0:T(8,128)} %scores.1.x_ref), custom_call_target="tpu_custom_call" | custom-call | tf_op jit(solution)/shard_map/stats/pallas_call | solution.py:637
  174.9 1.1 dynamic-slice_reduce_fusion
  176.1 0.1 sub.43
  176.1 0.0 copy-done.3
  176.1 0.1 dynamic_slice.9
  176.2 0.9 slice_reduce_fusion
  177.1 0.1 mul.39
  177.2 0.2 fusion.3
  177.4 0.0 copy-done.5
  177.4 0.8 fusion.4
  178.2 0.0 copy-done.4
  178.2 0.5 convert_divide_fusion
  (7 shorter events, 0.1 us)
Async XLA Ops:
  0.6 88.6 %copy-start = (bf16[2560,160]{0,1:T(8,128)(2,1)S(1)}, bf16[2560,160]{0,1:T(8,128)(2,1)}, u32[]{:S(2)}) copy-start(bf16[2560,160]{0,1:T(8,128)(2,1)} %param.22) | copy-start | bytes 2457604
  3.6 0.6 copy-start.1
  47.9 48.0 %copy-start.2 = (f32[2560]{0:T(1024)S(1)}, f32[2560]{0:T(1024)}, u32[]{:S(2)}) copy-start(f32[2560]{0:T(1024)} %param.23) | copy-start | bytes 30724
  97.3 78.8 %copy-start.3 = (s32[32]{0:T(128)S(1)}, s32[32]{0:T(128)}, u32[]{:S(2)}) copy-start(s32[32]{0:T(128)} %param.28) | copy-start | bytes 388
  97.3 80.1 %copy-start.5 = (s32[2]{0:T(128)S(1)}, s32[2]{0:T(128)}, u32[]{:S(2)}) copy-start(s32[2]{0:T(128)} %param.26) | copy-start | bytes 28
  97.3 80.8 %copy-start.4 = (f32[2]{0:T(128)S(1)}, f32[2]{0:T(128)}, u32[]{:S(2)}) copy-start(f32[2]{0:T(128)} %param.29) | copy-start | bytes 28
